TPU v7x, 256 devices: a whole 4x4x8 slice. The times are simulated.
256 devices in a mesh: gx: 8 (over z), gy: 4 (over y), gz: 8 (over x, core).
Axes of the slice: x: 4, y: 4, z: 8, core: 2. Of those that a mesh axis runs over, the one named last changes fastest.
Arguments:
- point_data: float32 [1, 6, 131072], P(None, None, ('gx', 'gy', 'gz')), may hold values from -1 to 1
- neighbours: int32 [1, 64, 64, 64, 32], P(None, 'gx', 'gy', 'gz'), may hold values from 0 to 131071, as said below
- counts: int32 [1, 64, 64, 64], P(None, 'gx', 'gy', 'gz'), may hold values from 1 to 32, as said below
- kernel_in: bfloat16 [6, 80], replicated, may hold values from -2.5 to 2.5
- kernel_mid: bfloat16 [80, 80], replicated, may hold values from -0.625 to 0.625
- kernel_out: bfloat16 [80, 64], replicated, may hold values from -0.625 to 0.625
- spectral: bfloat16 [2, 16, 16, 16, 64, 64], P(None, 'gz', 'gx', 'gy'), may hold values from -48 to 48
- skip_weight: bfloat16 [64, 64], replicated, may hold values from -0.75 to 0.75
Outputs:
- latent_out: float32 [1, 64, 64, 64, 64], P(None, 'gx', 'gy', 'gz')
Inputs may be any that keep to these rules, and one draw needn't show every extreme that they name: `neighbours`: points are owned by location: point j of a geometry belongs to the device at position j // 512 in the order gx, gy, gz. Every neighbour of a node is owned by the node's own device or by a device whose gx, gy and gz indices each differ from it by at most one. Slots s >= counts of the node are padding that names some point all the same. `counts`: on every device some node of every geometry has all 32 slots valid.
All inputs are finite; a program needn't handle non-finite values.
Results may differ from a plain program's by a relative error of at most 0.02.
Values may be sent and summed in bfloat16 or wider, within the bound.
A program may use at most 64 MiB of HBM per device.

v0:
```python
import functools
import math

import jax
import jax.numpy as jnp
from jax import lax
from jax.experimental import pallas as pl
from jax.experimental.pallas import tpu as pltpu
from jax.sharding import PartitionSpec as P

GRID = 64
MODES = 16
NB = 32


HIGH = lax.Precision.HIGH
NORM_FLOOR = 1.0


def extended(cells, sides, width):
    for axis, dim in sides:
        count = lax.axis_size(axis)
        ends = count - 1
        head = lax.slice_in_dim(cells, 0, width, axis=dim)
        tail = lax.slice_in_dim(cells, cells.shape[dim] - width, cells.shape[dim], axis=dim)
        cells = jnp.concatenate(
            [
                lax.ppermute(tail, axis, [(i, (i + 1) % count) for i in range(ends)]),
                cells,
                lax.ppermute(head, axis, [((i + 1) % count, i) for i in range(ends)]),
            ],
            axis=dim,
        )
    return cells


def tables(length, keep_count, centred):
    position = jnp.arange(length, dtype=jnp.int32)
    frequency = jnp.arange(keep_count, dtype=jnp.int32)
    if centred:
        frequency = jnp.where(
            frequency < keep_count // 2, frequency, frequency + length - keep_count
        )
    phases = frequency[:, None] * position[None, :] % length
    angles = phases.astype(jnp.float32) * (2.0 * math.pi / length)
    return (jnp.cos(angles), jnp.sin(angles))


def third_weights(cos_table, sin_table, length):
    factor = (
        jnp.where(jnp.arange(cos_table.shape[0]) == 0, 1.0, 2.0).astype(jnp.float32)[:, None]
        / length**3
    )
    return (cos_table * factor, sin_table * factor)


def contract(pattern, operand, table):
    return jnp.einsum(pattern, operand, table, precision=HIGH)


def forward_real(values, cos_table, sin_table, pattern):
    return (contract(pattern, values, cos_table), -contract(pattern, values, sin_table))


def forward_complex(real_part, imag_part, cos_table, sin_table, pattern):
    new_real = contract(pattern, real_part, cos_table) + contract(pattern, imag_part, sin_table)
    new_imag = contract(pattern, imag_part, cos_table) - contract(pattern, real_part, sin_table)
    return (new_real, new_imag)


def inverse_complex(real_part, imag_part, cos_table, sin_table, pattern):
    new_real = contract(pattern, real_part, cos_table) - contract(pattern, imag_part, sin_table)
    new_imag = contract(pattern, real_part, sin_table) + contract(pattern, imag_part, cos_table)
    return (new_real, new_imag)


def inverse_real(real_part, imag_part, cos_table, sin_table, pattern):
    return contract(pattern, real_part, cos_table) - contract(pattern, imag_part, sin_table)


def gelu(v):
    inner = v * (0.7978845608028654 + 0.035677408136300125 * (v * v))
    half = 0.5 * v
    return half + half * jnp.tanh(inner)


def encoder_kernel(
    blocks, slots_ref, blocks_ref, counts_ref, centres_ref, table_ref, first_ref, mid_ref, last_ref, out_ref, total
):
    width = slots_ref.shape[1]
    per_device = table_ref.shape[1]
    rest_rows = table_ref.shape[0] - 8 * blocks
    slot_ids = lax.broadcasted_iota(jnp.int32, (per_device, width), 0).astype(jnp.int16)
    rest_ids = lax.broadcasted_iota(jnp.int32, (rest_rows, width), 0)
    rows = lax.broadcasted_iota(jnp.int32, (8, width), 0)
    counts = counts_ref[...]
    centres = centres_ref[...]
    total[...] = jnp.zeros_like(total)

    def step(s, carry):
        slot = jnp.broadcast_to(slots_ref[pl.ds(s, 1), :], (16, width)).astype(jnp.int16)
        slot = jnp.concatenate([slot] * (per_device // 16), axis=0)
        hot = jnp.where(slot_ids == slot, jnp.bfloat16(1), jnp.bfloat16(0))
        found = jnp.dot(table_ref[...], hot, preferred_element_type=jnp.float32)
        block = blocks_ref[pl.ds(s, 1), :]
        wide = jnp.broadcast_to(block, (8, width))
        picked = found[0:8]
        for b in range(1, blocks):
            picked = jnp.where(wide == b, found[8 * b : 8 * b + 8], picked)
        third = jnp.sum(jnp.where(rest_ids == block, found[8 * blocks :], 0.0), axis=0, keepdims=True)
        place = picked + pltpu.roll(picked, 4, 0) - centres
        pair = jnp.where(rows < 3, place, jnp.where(rows == 4, third, picked)).astype(jnp.bfloat16)
        hidden = gelu(jnp.dot(first_ref[...], pair, preferred_element_type=jnp.float32))
        hidden = gelu(
            jnp.dot(mid_ref[...], hidden.astype(jnp.bfloat16), preferred_element_type=jnp.float32)
        )
        hidden = hidden.astype(jnp.bfloat16).astype(jnp.float32)
        total[...] += jnp.where(s < counts, hidden, 0.0)
        return carry

    lax.fori_loop(0, slots_ref.shape[0], step, 0, unroll=8)
    mean = total[...] / counts.astype(jnp.float32)
    upper = mean.astype(jnp.bfloat16)
    lower = (mean - upper.astype(jnp.float32)).astype(jnp.bfloat16)
    last = last_ref[...]
    values = jnp.dot(last, upper, preferred_element_type=jnp.float32) + jnp.dot(
        last, lower, preferred_element_type=jnp.float32
    )
    out_ref[...] = values.T.astype(jnp.bfloat16)


def encode(slots, block_ids, counts, centres, table, first, mid, last):
    nodes = slots.shape[1]
    width = min(512, nodes)
    channels = last.shape[0]
    tile = lambda rows: pl.BlockSpec((rows, width), lambda i: (0, i))
    whole = lambda array: pl.BlockSpec(array.shape, lambda i: (0, 0))
    return pl.pallas_call(
        functools.partial(encoder_kernel, 27),
        grid=(nodes // width,),
        out_shape=jax.ShapeDtypeStruct((nodes, channels), jnp.bfloat16),
        in_specs=[tile(NB), tile(NB), tile(1), tile(8), whole(table), whole(first), whole(mid), whole(last)],
        out_specs=pl.BlockSpec((width, channels), lambda i: (i, 0)),
        scratch_shapes=[pltpu.VMEM((mid.shape[0], width), jnp.float32)],
    )(slots, block_ids, counts, centres, table, first, mid, last)


def summed_over_axes(values, axes):
    for axis in axes:
        count = lax.axis_size(axis)
        copies = jnp.broadcast_to(values[None], (count,) + values.shape)
        values = jnp.sum(lax.all_to_all(copies, axis, 0, 0, tiled=True), axis=0)
    return values


def packed_table(table):
    upper = table.astype(jnp.bfloat16)
    lower = (table - upper.astype(jnp.float32)).astype(jnp.bfloat16)
    main = jnp.concatenate([upper[0:3], upper[3:4], lower[0:3], upper[4:5]], axis=0)
    main = jnp.transpose(main, (1, 0, 2)).reshape(-1, table.shape[2])
    rows = jnp.concatenate([main, upper[5]], axis=0)
    return jnp.pad(rows, ((0, -rows.shape[0] % 128), (0, 0)))


def exchange(values, axis, split_axis, concat_axis):
    return lax.all_to_all(
        values.astype(jnp.bfloat16), axis, split_axis=split_axis, concat_axis=concat_axis, tiled=True
    ).astype(jnp.float32)


def body(point_data, neighbours, counts, kernel_in, kernel_mid, kernel_out, spectral, skip_weight):
    count_y = lax.axis_size("gy")
    count_z = lax.axis_size("gz")
    place_x = lax.axis_index("gx")
    place_y = lax.axis_index("gy")
    place_z = lax.axis_index("gz")
    geometry_count, cells_x, cells_y, cells_z = neighbours.shape[0:4]
    per_device = point_data.shape[2]
    channels = skip_weight.shape[0]
    beside_all = extended(point_data[None, None, None], (("gx", 0), ("gy", 1), ("gz", 2)), 1)
    table = jnp.transpose(beside_all, (3, 4, 0, 1, 2, 5)).reshape(
        geometry_count, point_data.shape[1], 27, per_device
    )
    owner = neighbours // per_device
    offset_z = owner % count_z - place_z + 1
    offset_y = owner // count_z % count_y - place_y + 1
    offset_x = owner // (count_z * count_y) - place_x + 1
    block_index = (offset_x * 3 + offset_y) * 3 + offset_z
    slot_index = neighbours % per_device
    centre_y = (
        (place_y * cells_y + jnp.arange(cells_y, dtype=jnp.int32)).astype(jnp.float32) + 0.5
    ) / GRID
    centre_z = (
        (place_z * cells_z + jnp.arange(cells_z, dtype=jnp.int32)).astype(jnp.float32) + 0.5
    ) / GRID
    centre_x = (
        (place_x * cells_x + jnp.arange(cells_x, dtype=jnp.int32)).astype(jnp.float32) + 0.5
    ) / GRID
    shape = (cells_x, cells_y, cells_z)
    centres = jnp.stack(
        [
            jnp.broadcast_to(centre_x[:, None, None], shape).reshape(-1),
            jnp.broadcast_to(centre_y[None, :, None], shape).reshape(-1),
            jnp.broadcast_to(centre_z[None, None, :], shape).reshape(-1),
        ]
    )
    centres = jnp.pad(centres, ((0, 5), (0, 0)))
    first = jnp.stack(
        [kernel_in[0], kernel_in[1], kernel_in[2], kernel_in[3], kernel_in[5]]
        + [jnp.zeros_like(kernel_in[0])] * 2
        + [kernel_in[4]],
        axis=1,
    )
    code = (block_index * per_device + slot_index).reshape(geometry_count, -1, NB)
    latent = []
    for geometry in range(geometry_count):
        turned = code[geometry].T
        latent.append(
            encode(
                turned % per_device,
                turned // per_device,
                counts[geometry].reshape(1, -1),
                centres,
                packed_table(table[geometry]),
                first,
                kernel_mid.T,
                kernel_out.T,
            )
        )
    latent = jnp.stack(latent)
    latent = latent.reshape(geometry_count, cells_x, cells_y, cells_z, channels)
    cos_centred, sin_centred = tables(GRID, MODES, True)
    cos_third, sin_third = tables(GRID, MODES, False)
    back_cos, back_sin = third_weights(cos_third, sin_third, GRID)
    depth_full = lax.all_to_all(latent, "gz", split_axis=4, concat_axis=3, tiled=True)
    real_part, imag_part = forward_real(
        depth_full.astype(jnp.float32), cos_third, sin_third, "gxyzc,kz->gxykc"
    )
    real_part, imag_part = (
        lax.all_to_all(real_part, "gy", split_axis=3, concat_axis=2, tiled=True),
        lax.all_to_all(imag_part, "gy", split_axis=3, concat_axis=2, tiled=True),
    )
    real_part, imag_part = forward_complex(
        real_part, imag_part, cos_centred, sin_centred, "gxykc,jy->gxjkc"
    )
    real_part, imag_part = (
        lax.all_to_all(real_part, "gx", split_axis=2, concat_axis=1, tiled=True),
        lax.all_to_all(imag_part, "gx", split_axis=2, concat_axis=1, tiled=True),
    )
    real_part, imag_part = forward_complex(
        real_part, imag_part, cos_centred, sin_centred, "gxjkc,ix->gijkc"
    )
    spec_real, spec_imag = (
        exchange(real_part, "gz", split_axis=1, concat_axis=4),
        exchange(imag_part, "gz", split_axis=1, concat_axis=4),
    )
    spec_real = spec_real.astype(jnp.bfloat16)
    spec_imag = spec_imag.astype(jnp.bfloat16)
    mixed_real = jnp.einsum(
        "gijkc,ijkco->gijko", spec_real, spectral[0], preferred_element_type=jnp.float32
    ) - jnp.einsum("gijkc,ijkco->gijko", spec_imag, spectral[1], preferred_element_type=jnp.float32)
    mixed_imag = jnp.einsum(
        "gijkc,ijkco->gijko", spec_real, spectral[1], preferred_element_type=jnp.float32
    ) + jnp.einsum("gijkc,ijkco->gijko", spec_imag, spectral[0], preferred_element_type=jnp.float32)
    first_place = (place_x + place_y + place_z) == 0
    modes = mixed_real.shape[1:4]
    order = sum(lax.broadcasted_iota(jnp.int32, modes, d) for d in range(3))
    zero_mode = ((order == 0) & first_place)[None, ..., None]
    mixed_real = jnp.where(zero_mode, 0.0, mixed_real)
    mixed_imag = jnp.where(zero_mode, 0.0, mixed_imag)
    mixed_real = mixed_real.astype(jnp.bfloat16)
    mixed_imag = mixed_imag.astype(jnp.bfloat16)
    real_part, imag_part = (
        exchange(mixed_real, "gz", split_axis=4, concat_axis=1),
        exchange(mixed_imag, "gz", split_axis=4, concat_axis=1),
    )
    real_part, imag_part = inverse_complex(
        real_part.astype(jnp.float32),
        imag_part.astype(jnp.float32),
        cos_centred,
        sin_centred,
        "gijkc,ix->gxjkc",
    )
    real_part, imag_part = (
        exchange(real_part, "gx", split_axis=1, concat_axis=2),
        exchange(imag_part, "gx", split_axis=1, concat_axis=2),
    )
    real_part, imag_part = inverse_complex(
        real_part, imag_part, cos_centred, sin_centred, "gxjkc,jy->gxykc"
    )
    real_part, imag_part = (
        exchange(real_part, "gy", split_axis=2, concat_axis=3),
        exchange(imag_part, "gy", split_axis=2, concat_axis=3),
    )
    depth_part = inverse_real(real_part, imag_part, back_cos, back_sin, "gxykc,kz->gxyzc")
    branch = exchange(depth_part, "gz", split_axis=3, concat_axis=4)
    skip = jnp.einsum("gxyzc,co->gxyzo", latent, skip_weight, preferred_element_type=jnp.float32)
    cells_total = float(GRID**3)
    variance = (
        summed_over_axes(jnp.sum(branch * branch, axis=(1, 2, 3)), ("gz", "gy", "gx")) / cells_total
    )
    normed = branch / jnp.sqrt(variance + NORM_FLOOR)[:, None, None, None, :]
    return jax.nn.gelu(normed + skip, approximate=True)


def solution(mesh):
    in_specs = (
        P(None, None, ("gx", "gy", "gz")),
        P(None, "gx", "gy", "gz", None),
        P(None, "gx", "gy", "gz"),
        P(),
        P(),
        P(),
        P(None, "gz", "gx", "gy", None, None),
        P(),
    )
    out_specs = P(None, "gx", "gy", "gz", None)
    return jax.shard_map(body, mesh=mesh, in_specs=in_specs, out_specs=out_specs, check_vma=False)
```

profile of v0, /device:TPU:1, one launch (start us, length us, event | category | flops | bytes accessed | tf_op | source)
XLA Modules:
  0.0 259.2 jit_solution(4510865854020265527)
XLA Ops:
  1.5 5.0 %collective-permute-start = (f32[1,1,1,1,6,512]{5,0,4,3,2,1:T(1,128)}, f32[1,1,1,1,6,512]{5,0,4,3,2,1:T(1,128)S(1)}, u32[]{:S(2)}, u32[]{:S(2)}) collective-permute-start(f32[1,1,1,1,6,512]{5,0,4,3,2,1:T(1,128)} %bitcast.386), channel_id=1, source_target_pairs={{0,32},{32,64},{64,96},{96,128},{128,160},{160,192},{192,224},{1,3... | collective-permute-start | bytes 36872 | tf_op jit(solution)/shard_map/ppermute | solution.py:28
  12.3 4.0 %collective-permute-start.2 = (f32[3,1,1,1,6,512]{5,0,4,3,2,1:T(4,128)S(1)}, f32[3,1,1,1,6,512]{5,0,4,3,2,1:T(4,128)S(1)}, u32[]{:S(2)}, u32[]{:S(2)}) collective-permute-start(f32[3,1,1,1,6,512]{5,0,4,3,2,1:T(4,128)S(1)} %pad_maximum_fusion.1), channel_id=1, source_target_pairs={{0,8},{8,16},{16,24},{1,9},{9,17},{17,25},{2,10},{10,18},{18,26},{... | collective-permute-start | bytes 110600 | tf_op jit(solution)/shard_map/ppermute | solution.py:28
  19.0 5.2 %collective-permute-start.5 = (f32[3,3,1,1,6,512]{5,0,4,3,2,1:T(4,128)S(1)}, f32[3,3,1,1,6,512]{5,0,4,3,2,1:T(4,128)S(1)}, u32[]{:S(2)}, u32[]{:S(2)}) collective-permute-start(f32[3,3,1,1,6,512]{5,0,4,3,2,1:T(4,128)S(1)} %pad_maximum_fusion), channel_id=1, source_target_pairs={{1,0},{2,1},{3,2},{4,3},{5,4},{6,5},{7,6},{9,8},{10,9},{11,10},{12... | collective-permute-start | bytes 331784 | tf_op jit(solution)/shard_map/ppermute | solution.py:30
  29.7 35.6 %shard_map.82 = bf16[1024,64]{1,0:T(8,128)(2,1)} custom-call(s32[32,1024]{1,0:T(8,128)} %get-tuple-element.10.slots_ref, s32[32,1024]{1,0:T(8,128)} %get-tuple-element.9.blocks_ref, s32[1,1024]{1,0:T(1,128)} %reshape_squeeze.3.counts_ref, f32[8,1024]{1,0:T(8,128)} %select_maximum_fusion.centres_ref, bf16[256,512]{1,0:T(8,128)(2,1)} %fusion.30.table_ref, ...), custom_call_target="tpu_custom_call" | custom-call | tf_op jit(solution)/shard_map/pallas_call | solution.py:138
  69.8 5.1 %all-to-all-start = ((bf16[8,2,4096]{2,1,0:T(2,128)(2,1)}), bf16[8,2,4096]{2,1,0:T(2,128)(2,1)S(1)}, u32[]{:S(2)}, u32[]{:S(2)}) async-start(bf16[8,2,4096]{2,1,0:T(2,128)(2,1)} %reshape.313), calls=%async_computation | async-start | bytes 262144 | tf_op jit(solution)/shard_map/all_to_all | solution.py:235
  74.9 5.2 %all-to-all-done = bf16[8,2,4096]{2,1,0:T(2,128)(2,1)S(1)} async-done(((bf16[8,2,4096]{2,1,0:T(2,128)(2,1)}), bf16[8,2,4096]{2,1,0:T(2,128)(2,1)S(1)}, u32[]{:S(2)}, u32[]{:S(2)}) %all-to-all-start) | async-done | bytes 131104 | tf_op jit(solution)/shard_map/all_to_all | solution.py:235
  84.8 4.2 %all-to-all-start.1 = ((f32[4,1,4096]{2,1,0:T(1,128)}), f32[4,1,4096]{2,1,0:T(1,128)S(1)}, u32[]{:S(2)}, u32[]{:S(2)}) async-start(f32[4,1,4096]{2,1,0:T(1,128)} %reshape.317), calls=%async_computation.1 | async-start | bytes 131072 | tf_op jit(solution)/shard_map/all_to_all | solution.py:240
  104.5 8.2 %all-to-all-start.3 = ((f32[8,1,512]{2,1,0:T(1,128)}), f32[8,1,512]{2,1,0:T(1,128)S(1)}, u32[]{:S(2)}, u32[]{:S(2)}) async-start(f32[8,1,512]{2,1,0:T(1,128)} %reshape.321), calls=%async_computation.3 | async-start | bytes 32768 | tf_op jit(solution)/shard_map/all_to_all | solution.py:247
  113.9 5.4 %all-to-all-done.3 = f32[8,1,512]{2,1,0:T(1,128)S(1)} async-done(((f32[8,1,512]{2,1,0:T(1,128)}), f32[8,1,512]{2,1,0:T(1,128)S(1)}, u32[]{:S(2)}, u32[]{:S(2)}) %all-to-all-start.3) | async-done | bytes 16416 | tf_op jit(solution)/shard_map/all_to_all | solution.py:247
  119.3 3.3 %all-to-all-start.4 = ((f32[8,1,512]{2,1,0:T(1,128)}), f32[8,1,512]{2,1,0:T(1,128)S(1)}, u32[]{:S(2)}, u32[]{:S(2)}) async-start(f32[8,1,512]{2,1,0:T(1,128)} %reshape.319), calls=%async_computation.4 | async-start | bytes 32768 | tf_op jit(solution)/shard_map/all_to_all | solution.py:248
  124.5 4.8 %all-to-all-done.4 = f32[8,1,512]{2,1,0:T(1,128)S(1)} async-done(((f32[8,1,512]{2,1,0:T(1,128)}), f32[8,1,512]{2,1,0:T(1,128)S(1)}, u32[]{:S(2)}, u32[]{:S(2)}) %all-to-all-start.4) | async-done | bytes 16416 | tf_op jit(solution)/shard_map/all_to_all | solution.py:248
  131.7 9.3 %all-to-all-start.6 = ((bf16[1,16,2,4,8]{4,3,2,0,1:T(4,128)(2,1)}), bf16[1,16,2,4,8]{4,3,2,0,1:T(4,128)(2,1)S(1)}, u32[]{:S(2)}, u32[]{:S(2)}) async-start(bf16[1,16,2,4,8]{4,3,2,0,1:T(4,128)(2,1)} %copy.412), calls=%async_computation.6 | async-start | bytes 65536 | tf_op jit(solution)/shard_map/all_to_all | solution.py:166
  141.7 4.0 %all-to-all-done.6 = bf16[1,16,2,4,8]{4,3,2,0,1:T(4,128)(2,1)S(1)} async-done(((bf16[1,16,2,4,8]{4,3,2,0,1:T(4,128)(2,1)}), bf16[1,16,2,4,8]{4,3,2,0,1:T(4,128)(2,1)S(1)}, u32[]{:S(2)}, u32[]{:S(2)}) %all-to-all-start.6) | async-done | bytes 2080 | tf_op jit(solution)/shard_map/all_to_all | solution.py:166
  145.8 4.0 %all-to-all-start.5 = ((bf16[1,16,2,4,8]{4,3,2,0,1:T(4,128)(2,1)}), bf16[1,16,2,4,8]{4,3,2,0,1:T(4,128)(2,1)S(1)}, u32[]{:S(2)}, u32[]{:S(2)}) async-start(bf16[1,16,2,4,8]{4,3,2,0,1:T(4,128)(2,1)} %copy.409), calls=%async_computation.5 | async-start | bytes 65536 | tf_op jit(solution)/shard_map/all_to_all | solution.py:166
  150.2 4.2 %all-to-all-done.5 = bf16[1,16,2,4,8]{4,3,2,0,1:T(4,128)(2,1)S(1)} async-done(((bf16[1,16,2,4,8]{4,3,2,0,1:T(4,128)(2,1)}), bf16[1,16,2,4,8]{4,3,2,0,1:T(4,128)(2,1)S(1)}, u32[]{:S(2)}, u32[]{:S(2)}) %all-to-all-start.5) | async-done | bytes 2080 | tf_op jit(solution)/shard_map/all_to_all | solution.py:166
  156.4 7.9 %all_to_all.219 = bf16[1,2,2,4,64]{3,2,1,0,4:T(2,128)(2,1)S(1)} all-to-all(bf16[1,2,2,4,64]{3,2,1,0,4:T(2,128)(2,1)S(1)} %get-tuple-element.18), channel_id=1, replica_groups=mesh['gx'=8,'gy'=4,'gz'=8] {'gz'}, dimensions={4} | all-to-all | bytes 4096 | tf_op jit(solution)/shard_map/all_to_all | solution.py:166
  164.3 4.0 %all-to-all-start.8 = ((bf16[1,2,2,4,64]{3,2,1,0,4:T(2,128)(2,1)}), bf16[1,2,2,4,64]{3,2,1,0,4:T(2,128)(2,1)S(1)}, u32[]{:S(2)}, u32[]{:S(2)}) async-start(bf16[1,2,2,4,64]{3,2,1,0,4:T(2,128)(2,1)} %get-tuple-element.17), calls=%async_computation.8 | async-start | bytes 131072 | tf_op jit(solution)/shard_map/all_to_all | solution.py:166
  169.3 3.9 %all-to-all-done.8 = bf16[1,2,2,4,64]{3,2,1,0,4:T(2,128)(2,1)S(1)} async-done(((bf16[1,2,2,4,64]{3,2,1,0,4:T(2,128)(2,1)}), bf16[1,2,2,4,64]{3,2,1,0,4:T(2,128)(2,1)S(1)}, u32[]{:S(2)}, u32[]{:S(2)}) %all-to-all-start.8) | async-done | bytes 2080 | tf_op jit(solution)/shard_map/all_to_all | solution.py:166
  179.3 5.6 %all-to-all-done.9 = bf16[8,2,256]{2,1,0:T(2,128)(2,1)S(1)} async-done(((bf16[8,2,256]{2,1,0:T(2,128)(2,1)}), bf16[8,2,256]{2,1,0:T(2,128)(2,1)S(1)}, u32[]{:S(2)}, u32[]{:S(2)}) %all-to-all-start.9) | async-done | bytes 8224 | tf_op jit(solution)/shard_map/all_to_all | solution.py:166
  189.3 5.5 %all-to-all-done.10 = bf16[8,2,256]{2,1,0:T(2,128)(2,1)S(1)} async-done(((bf16[8,2,256]{2,1,0:T(2,128)(2,1)}), bf16[8,2,256]{2,1,0:T(2,128)(2,1)S(1)}, u32[]{:S(2)}, u32[]{:S(2)}) %all-to-all-start.10) | async-done | bytes 8224 | tf_op jit(solution)/shard_map/all_to_all | solution.py:166
  197.7 3.5 %all-to-all-start.12 = ((bf16[4,2,2048]{2,1,0:T(2,128)(2,1)}), bf16[4,2,2048]{2,1,0:T(2,128)(2,1)S(1)}, u32[]{:S(2)}, u32[]{:S(2)}) async-start(bf16[4,2,2048]{2,1,0:T(2,128)(2,1)} %reshape.329), calls=%async_computation.12 | async-start | bytes 65536 | tf_op jit(solution)/shard_map/all_to_all | solution.py:166
  217.8 13.0 %all_to_all.220 = bf16[8,2,4096]{2,1,0:T(2,128)(2,1)S(1)} all-to-all(bf16[8,2,4096]{2,1,0:T(2,128)(2,1)S(1)} %reshape.331), channel_id=1, replica_groups=mesh['gx'=8,'gy'=4,'gz'=8] {'gz'}, dimensions={0} | all-to-all | bytes 262144 | tf_op jit(solution)/shard_map/all_to_all | solution.py:166
  233.2 7.8 %all_to_all.221 = f32[8,1,64]{2,1,0:T(1,128)S(1)} all-to-all(f32[8,1,64]{2,1,0:T(1,128)S(1)} %broadcast_in_dim.81), channel_id=1, replica_groups=mesh['gx'=8,'gy'=4,'gz'=8] {'gz'}, dimensions={0} | all-to-all | bytes 4096 | tf_op jit(solution)/shard_map/all_to_all | solution.py:152
  241.0 6.5 %all_to_all.222 = f32[4,1,64]{2,1,0:T(1,128)S(1)} all-to-all(f32[4,1,64]{2,1,0:T(1,128)S(1)} %broadcast_in_dim.82), channel_id=1, replica_groups=mesh['gx'=8,'gy'=4,'gz'=8] {'gy'}, dimensions={0} | all-to-all | bytes 2048 | tf_op jit(solution)/shard_map/all_to_all | solution.py:152
  (190 shorter events, 93.0 us)
Async XLA Ops:
  0.0 257.9 %copy-start = (bf16[64,64]{1,0:T(8,128)(2,1)S(1)}, bf16[64,64]{1,0:T(8,128)(2,1)}, u32[]{:S(2)}) copy-start(bf16[64,64]{1,0:T(8,128)(2,1)} %param.15) | copy-start | bytes 24580
  0.0 10.9 %copy-start.2 = (f32[1,6,512]{2,0,1:T(1,128)S(1)}, f32[1,6,512]{2,0,1:T(1,128)}, u32[]{:S(2)}) copy-start(f32[1,6,512]{2,0,1:T(1,128)} %param.8) | copy-start | bytes 36868
  0.0 17.0 %copy-start.4 = (bf16[80,80]{1,0:T(8,128)(2,1)S(1)}, bf16[80,80]{1,0:T(8,128)(2,1)}, u32[]{:S(2)}) copy-start(bf16[80,80]{1,0:T(8,128)(2,1)} %param.12) | copy-start | bytes 38404
  0.0 18.2 %copy-start.3 = (s32[1,8,16,8]{2,3,1,0:T(8,128)S(1)}, s32[1,8,16,8]{2,3,1,0:T(8,128)}, u32[]{:S(2)}) copy-start(s32[1,8,16,8]{2,3,1,0:T(8,128)} %param.10) | copy-start | bytes 12292
  0.0 10.9 %collective-permute-start.1 = (f32[1,1,1,1,6,512]{5,0,4,3,2,1:T(1,128)}, f32[1,1,1,1,6,512]{5,0,4,3,2,1:T(1,128)S(1)}, u32[]{:S(2)}, u32[]{:S(2)}) collective-permute-start(f32[1,1,1,1,6,512]{5,0,4,3,2,1:T(1,128)} %bitcast.385), channel_id=1, source_target_pairs={{32,0},{64,32},{96,64},{128,96},{160,128},{192,160},{224,192},{33,... | collective-permute-start | bytes 36872 | tf_op jit(solution)/shard_map/ppermute | solution.py:30
  1.5 9.4 %collective-permute-start = (f32[1,1,1,1,6,512]{5,0,4,3,2,1:T(1,128)}, f32[1,1,1,1,6,512]{5,0,4,3,2,1:T(1,128)S(1)}, u32[]{:S(2)}, u32[]{:S(2)}) collective-permute-start(f32[1,1,1,1,6,512]{5,0,4,3,2,1:T(1,128)} %bitcast.386), channel_id=1, source_target_pairs={{0,32},{32,64},{64,96},{96,128},{128,160},{160,192},{192,224},{1,3... | collective-permute-start | bytes 36872 | tf_op jit(solution)/shard_map/ppermute | solution.py:28
  11.0 8.0 %collective-permute-start.3 = (f32[3,1,1,1,6,512]{5,0,4,3,2,1:T(4,128)S(1)}, f32[3,1,1,1,6,512]{5,0,4,3,2,1:T(4,128)S(1)}, u32[]{:S(2)}, u32[]{:S(2)}) collective-permute-start(f32[3,1,1,1,6,512]{5,0,4,3,2,1:T(4,128)S(1)} %pad_maximum_fusion.1), channel_id=1, source_target_pairs={{8,0},{16,8},{24,16},{9,1},{17,9},{25,17},{10,2},{18,10},{26,18},{... | collective-permute-start | bytes 110600 | tf_op jit(solution)/shard_map/ppermute | solution.py:30
  12.3 6.7 %collective-permute-start.2 = (f32[3,1,1,1,6,512]{5,0,4,3,2,1:T(4,128)S(1)}, f32[3,1,1,1,6,512]{5,0,4,3,2,1:T(4,128)S(1)}, u32[]{:S(2)}, u32[]{:S(2)}) collective-permute-start(f32[3,1,1,1,6,512]{5,0,4,3,2,1:T(4,128)S(1)} %pad_maximum_fusion.1), channel_id=1, source_target_pairs={{0,8},{8,16},{16,24},{1,9},{9,17},{17,25},{2,10},{10,18},{18,26},{... | collective-permute-start | bytes 110600 | tf_op jit(solution)/shard_map/ppermute | solution.py:28
  19.0 7.8 %collective-permute-start.5 = (f32[3,3,1,1,6,512]{5,0,4,3,2,1:T(4,128)S(1)}, f32[3,3,1,1,6,512]{5,0,4,3,2,1:T(4,128)S(1)}, u32[]{:S(2)}, u32[]{:S(2)}) collective-permute-start(f32[3,3,1,1,6,512]{5,0,4,3,2,1:T(4,128)S(1)} %pad_maximum_fusion), channel_id=1, source_target_pairs={{1,0},{2,1},{3,2},{4,3},{5,4},{6,5},{7,6},{9,8},{10,9},{11,10},{12... | collective-permute-start | bytes 331784 | tf_op jit(solution)/shard_map/ppermute | solution.py:30
  24.3 4.0 %collective-permute-start.4 = (f32[3,3,1,1,6,512]{5,0,4,3,2,1:T(4,128)S(1)}, f32[3,3,1,1,6,512]{5,0,4,3,2,1:T(4,128)S(1)}, u32[]{:S(2)}, u32[]{:S(2)}) collective-permute-start(f32[3,3,1,1,6,512]{5,0,4,3,2,1:T(4,128)S(1)} %pad_maximum_fusion), channel_id=1, source_target_pairs={{0,1},{1,2},{2,3},{3,4},{4,5},{5,6},{6,7},{8,9},{9,10},{10,11},{11... | collective-permute-start | bytes 331784 | tf_op jit(solution)/shard_map/ppermute | solution.py:28
  69.8 10.3 %all-to-all-start = ((bf16[8,2,4096]{2,1,0:T(2,128)(2,1)}), bf16[8,2,4096]{2,1,0:T(2,128)(2,1)S(1)}, u32[]{:S(2)}, u32[]{:S(2)}) async-start(bf16[8,2,4096]{2,1,0:T(2,128)(2,1)} %reshape.313), calls=%async_computation | async-start | bytes 262144 | tf_op jit(solution)/shard_map/all_to_all | solution.py:235
  84.8 8.7 %all-to-all-start.1 = ((f32[4,1,4096]{2,1,0:T(1,128)}), f32[4,1,4096]{2,1,0:T(1,128)S(1)}, u32[]{:S(2)}, u32[]{:S(2)}) async-start(f32[4,1,4096]{2,1,0:T(1,128)} %reshape.317), calls=%async_computation.1 | async-start | bytes 131072 | tf_op jit(solution)/shard_map/all_to_all | solution.py:240
  93.4 7.7 %all-to-all-start.2 = ((f32[4,1,4096]{2,1,0:T(1,128)}), f32[4,1,4096]{2,1,0:T(1,128)S(1)}, u32[]{:S(2)}, u32[]{:S(2)}) async-start(f32[4,1,4096]{2,1,0:T(1,128)} %reshape.315), calls=%async_computation.2 | async-start | bytes 131072 | tf_op jit(solution)/shard_map/all_to_all | solution.py:241
  104.5 14.8 %all-to-all-start.3 = ((f32[8,1,512]{2,1,0:T(1,128)}), f32[8,1,512]{2,1,0:T(1,128)S(1)}, u32[]{:S(2)}, u32[]{:S(2)}) async-start(f32[8,1,512]{2,1,0:T(1,128)} %reshape.321), calls=%async_computation.3 | async-start | bytes 32768 | tf_op jit(solution)/shard_map/all_to_all | solution.py:247
  113.9 35.9 %copy-start.5 = (bf16[2,2,2,4,64,64]{5,4,3,2,1,0:T(8,128)(2,1)S(1)}, bf16[2,2,2,4,64,64]{5,4,3,2,1,0:T(8,128)(2,1)}, u32[]{:S(2)}) copy-start(bf16[2,2,2,4,64,64]{5,4,3,2,1,0:T(8,128)(2,1)} %param.14) | copy-start | bytes 786436
  119.3 9.9 %all-to-all-start.4 = ((f32[8,1,512]{2,1,0:T(1,128)}), f32[8,1,512]{2,1,0:T(1,128)S(1)}, u32[]{:S(2)}, u32[]{:S(2)}) async-start(f32[8,1,512]{2,1,0:T(1,128)} %reshape.319), calls=%async_computation.4 | async-start | bytes 32768 | tf_op jit(solution)/shard_map/all_to_all | solution.py:248
  131.7 14.0 %all-to-all-start.6 = ((bf16[1,16,2,4,8]{4,3,2,0,1:T(4,128)(2,1)}), bf16[1,16,2,4,8]{4,3,2,0,1:T(4,128)(2,1)S(1)}, u32[]{:S(2)}, u32[]{:S(2)}) async-start(bf16[1,16,2,4,8]{4,3,2,0,1:T(4,128)(2,1)} %copy.412), calls=%async_computation.6 | async-start | bytes 65536 | tf_op jit(solution)/shard_map/all_to_all | solution.py:166
  145.8 8.7 %all-to-all-start.5 = ((bf16[1,16,2,4,8]{4,3,2,0,1:T(4,128)(2,1)}), bf16[1,16,2,4,8]{4,3,2,0,1:T(4,128)(2,1)S(1)}, u32[]{:S(2)}, u32[]{:S(2)}) async-start(bf16[1,16,2,4,8]{4,3,2,0,1:T(4,128)(2,1)} %copy.409), calls=%async_computation.5 | async-start | bytes 65536 | tf_op jit(solution)/shard_map/all_to_all | solution.py:166
  164.3 8.9 %all-to-all-start.8 = ((bf16[1,2,2,4,64]{3,2,1,0,4:T(2,128)(2,1)}), bf16[1,2,2,4,64]{3,2,1,0,4:T(2,128)(2,1)S(1)}, u32[]{:S(2)}, u32[]{:S(2)}) async-start(bf16[1,2,2,4,64]{3,2,1,0,4:T(2,128)(2,1)} %get-tuple-element.17), calls=%async_computation.8 | async-start | bytes 131072 | tf_op jit(solution)/shard_map/all_to_all | solution.py:166
  175.1 9.9 %all-to-all-start.9 = ((bf16[8,2,256]{2,1,0:T(2,128)(2,1)}), bf16[8,2,256]{2,1,0:T(2,128)(2,1)S(1)}, u32[]{:S(2)}, u32[]{:S(2)}) async-start(bf16[8,2,256]{2,1,0:T(2,128)(2,1)} %reshape.323), calls=%async_computation.9 | async-start | bytes 16384 | tf_op jit(solution)/shard_map/all_to_all | solution.py:166
  185.0 9.9 %all-to-all-start.10 = ((bf16[8,2,256]{2,1,0:T(2,128)(2,1)}), bf16[8,2,256]{2,1,0:T(2,128)(2,1)S(1)}, u32[]{:S(2)}, u32[]{:S(2)}) async-start(bf16[8,2,256]{2,1,0:T(2,128)(2,1)} %reshape.325), calls=%async_computation.10 | async-start | bytes 16384 | tf_op jit(solution)/shard_map/all_to_all | solution.py:166
  197.7 7.5 %all-to-all-start.12 = ((bf16[4,2,2048]{2,1,0:T(2,128)(2,1)}), bf16[4,2,2048]{2,1,0:T(2,128)(2,1)S(1)}, u32[]{:S(2)}, u32[]{:S(2)}) async-start(bf16[4,2,2048]{2,1,0:T(2,128)(2,1)} %reshape.329), calls=%async_computation.12 | async-start | bytes 65536 | tf_op jit(solution)/shard_map/all_to_all | solution.py:166
  205.3 7.5 %all-to-all-start.11 = ((bf16[4,2,2048]{2,1,0:T(2,128)(2,1)}), bf16[4,2,2048]{2,1,0:T(2,128)(2,1)S(1)}, u32[]{:S(2)}, u32[]{:S(2)}) async-start(bf16[4,2,2048]{2,1,0:T(2,128)(2,1)} %reshape.327), calls=%async_computation.11 | async-start | bytes 65536 | tf_op jit(solution)/shard_map/all_to_all | solution.py:166
  248.1 9.7 %all-to-all-start.16 = ((f32[8,1,64]{2,1,0:T(1,128)}), f32[8,1,64]{2,1,0:T(1,128)S(1)}, u32[]{:S(2)}, u32[]{:S(2)}) async-start(f32[8,1,64]{2,1,0:T(1,128)} %broadcast_in_dim.83), calls=%async_computation.16 | async-start | bytes 8192 | tf_op jit(solution)/shard_map/all_to_all | solution.py:152
  (1 other events, 2.8 us)
where the time goes:
time: 261 us; the launch traced here: 259 us
  starting transfers between devices  76.9 us (29%)
  waiting for transfers between devices  51.1 us (20%)
  local copies, waits for them, and re-layouts  41.5 us (16%)
  Pallas kernels  35.6 us (14%)
  blocking collectives  35.2 us (13%)
  other arithmetic  9.02 us (3%)
  matrix products  8.9 us (3%)
    pallas_call x1, Pallas kernels, encode(): pl.pallas_call(functools.partial(encoder_kernel, 27), grid=(nodes // widt...  35.6 us
    all_to_all x7, starting transfers between devices, exchange(): lax.all_to_all(values.astype(jnp.bfloat16), axis, split_axis=split_axis,...  30.7 us
    all_to_all x7, waiting for transfers between devices, exchange(): lax.all_to_all(values.astype(jnp.bfloat16), axis, split_axis=split_axis,...  28.2 us
    all_to_all x2, blocking collectives, exchange(): lax.all_to_all(values.astype(jnp.bfloat16), axis, split_axis=split_axis,...  20.9 us
    unnamed x36, local copies, waits for them, and re-layouts  15.1 us
    all_to_all x2, blocking collectives, summed_over_axes(): values = jnp.sum(lax.all_to_all(copies, axis, 0, 0, tiled=True), axis=0)  14.3 us
    ppermute x3, starting transfers between devices, extended(): lax.ppermute(tail, axis, [(i, (i + 1) % count) for i in range(ends)])  10.9 us
    all_to_all x1, starting transfers between devices, body(): lax.all_to_all(real_part, 'gx', split_axis=2, concat_axis=1, tiled=True)  8.19 us
  transfers between devices with their start and end apart: 19, of which 14 were waited for; matrix products, arithmetic and copies ran while one was open for 11% of the time, Pallas kernels for 0%

commit v1 on v0

v1 whole, which is shorter than its diff:
```python
import functools
import math

import jax
import jax.numpy as jnp
import ml_dtypes
import numpy as np
from jax import lax
from jax.experimental import pallas as pl
from jax.experimental.pallas import tpu as pltpu
from jax.sharding import PartitionSpec as P

GRID = 64
MODES = 16
NB = 32
NORM_FLOOR = 1.0
GX, GY, GZ = 8, 4, 8
F32 = jnp.float32
BF16 = jnp.bfloat16
MESH = pl.DeviceIdType.MESH


def extended(cells, sides, width):
    for axis, dim in sides:
        count = lax.axis_size(axis)
        ends = count - 1
        head = lax.slice_in_dim(cells, 0, width, axis=dim)
        tail = lax.slice_in_dim(cells, cells.shape[dim] - width, cells.shape[dim], axis=dim)
        cells = jnp.concatenate(
            [
                lax.ppermute(tail, axis, [(i, (i + 1) % count) for i in range(ends)]),
                cells,
                lax.ppermute(head, axis, [((i + 1) % count, i) for i in range(ends)]),
            ],
            axis=dim,
        )
    return cells


def gelu(v):
    inner = v * (0.7978845608028654 + 0.035677408136300125 * (v * v))
    half = 0.5 * v
    return half + half * jnp.tanh(inner)


def encoder_kernel(
    blocks, slots_ref, blocks_ref, counts_ref, centres_ref, table_ref, first_ref, mid_ref, last_ref, out_ref, total
):
    width = slots_ref.shape[1]
    per_device = table_ref.shape[1]
    rest_rows = table_ref.shape[0] - 8 * blocks
    slot_ids = lax.broadcasted_iota(jnp.int32, (per_device, width), 0).astype(jnp.int16)
    rest_ids = lax.broadcasted_iota(jnp.int32, (rest_rows, width), 0)
    rows = lax.broadcasted_iota(jnp.int32, (8, width), 0)
    counts = counts_ref[...]
    centres = centres_ref[...]
    total[...] = jnp.zeros_like(total)

    def step(s, carry):
        slot = jnp.broadcast_to(slots_ref[pl.ds(s, 1), :], (16, width)).astype(jnp.int16)
        slot = jnp.concatenate([slot] * (per_device // 16), axis=0)
        hot = jnp.where(slot_ids == slot, jnp.bfloat16(1), jnp.bfloat16(0))
        found = jnp.dot(table_ref[...], hot, preferred_element_type=jnp.float32)
        block = blocks_ref[pl.ds(s, 1), :]
        wide = jnp.broadcast_to(block, (8, width))
        picked = found[0:8]
        for b in range(1, blocks):
            picked = jnp.where(wide == b, found[8 * b : 8 * b + 8], picked)
        third = jnp.sum(jnp.where(rest_ids == block, found[8 * blocks :], 0.0), axis=0, keepdims=True)
        place = picked + pltpu.roll(picked, 4, 0) - centres
        pair = jnp.where(rows < 3, place, jnp.where(rows == 4, third, picked)).astype(jnp.bfloat16)
        hidden = gelu(jnp.dot(first_ref[...], pair, preferred_element_type=jnp.float32))
        hidden = gelu(
            jnp.dot(mid_ref[...], hidden.astype(jnp.bfloat16), preferred_element_type=jnp.float32)
        )
        hidden = hidden.astype(jnp.bfloat16).astype(jnp.float32)
        total[...] += jnp.where(s < counts, hidden, 0.0)
        return carry

    lax.fori_loop(0, slots_ref.shape[0], step, 0, unroll=8)
    mean = total[...] / counts.astype(jnp.float32)
    upper = mean.astype(jnp.bfloat16)
    lower = (mean - upper.astype(jnp.float32)).astype(jnp.bfloat16)
    last = last_ref[...]
    values = jnp.dot(last, upper, preferred_element_type=jnp.float32) + jnp.dot(
        last, lower, preferred_element_type=jnp.float32
    )
    tiles = width // 128
    parts = [values[:, 128 * t : 128 * t + 128].reshape(8, 8, 128) for t in range(tiles)]
    out_ref[...] = jnp.stack(parts, axis=1).reshape(8, 8 * tiles, 128).astype(jnp.bfloat16)


def encode(slots, block_ids, counts, centres, table, first, mid, last):
    nodes = slots.shape[1]
    width = min(512, nodes)
    tile = lambda rows: pl.BlockSpec((rows, width), lambda i: (0, i))
    whole = lambda array: pl.BlockSpec(array.shape, lambda i: (0, 0))
    return pl.pallas_call(
        functools.partial(encoder_kernel, 27),
        grid=(nodes // width,),
        out_shape=jax.ShapeDtypeStruct((8, nodes // 16, 128), jnp.bfloat16),
        in_specs=[tile(NB), tile(NB), tile(1), tile(8), whole(table), whole(first), whole(mid), whole(last)],
        out_specs=pl.BlockSpec((8, width // 16, 128), lambda i: (0, i, 0)),
        scratch_shapes=[pltpu.VMEM((mid.shape[0], width), jnp.float32)],
    )(slots, block_ids, counts, centres, table, first, mid, last)


def packed_table(table):
    upper = table.astype(jnp.bfloat16)
    lower = (table - upper.astype(jnp.float32)).astype(jnp.bfloat16)
    main = jnp.concatenate([upper[0:3], upper[3:4], lower[0:3], upper[4:5]], axis=0)
    main = jnp.transpose(main, (1, 0, 2)).reshape(-1, table.shape[2])
    rows = jnp.concatenate([main, upper[5]], axis=0)
    return jnp.pad(rows, ((0, -rows.shape[0] % 128), (0, 0)))


def halves(values):
    upper = values.astype(np.float32).astype(ml_dtypes.bfloat16)
    lower = (values - upper.astype(np.float64)).astype(np.float32).astype(ml_dtypes.bfloat16)
    return np.stack([upper, lower])


def turn(frequency, position):
    angle = 2.0 * math.pi * ((frequency * position) % GRID) / GRID
    return np.cos(angle), np.sin(angle)


def centred(index):
    return np.where(index < MODES // 2, index, index - MODES)


def complex_block(cos, sin):
    return np.stack([np.stack([cos, sin], -1), np.stack([-sin, cos], -1)], -2)


@functools.lru_cache(None)
def third_table():
    cos, sin = turn(np.arange(16)[:, None], np.arange(64)[None, :])
    parts = np.stack([cos, -sin]).reshape(2, 4, 4, 64).transpose(1, 0, 2, 3)
    full = np.einsum("arkz,cd->arkczd", parts, np.eye(8))
    return full.reshape(256, 512)


@functools.lru_cache(None)
def second_table():
    j = np.arange(16)
    cos, sin = turn(centred(j)[:, None], np.arange(64)[None, :])
    both = complex_block(cos, sin).reshape(8, 2, 4, 16, 2, 2)
    full = np.einsum("gleyab,xw->lgaxebwy", both, np.eye(8))
    return full.reshape(2, 128, 1024)


@functools.lru_cache(None)
def first_table():
    i = np.arange(16)
    cos, sin = turn(centred(i)[:, None], np.arange(64)[None, :])
    both = complex_block(cos, sin).reshape(8, 2, 8, 8, 2, 2)
    full = np.einsum("hltxab,gf->tlghafbx", both, np.eye(8))
    return full.reshape(8, 2, 128, 128)


@functools.lru_cache(None)
def pair_table():
    out = np.zeros((4, 8, 8, 2, 8, 8, 2))
    for il in range(2):
        for jl in range(2):
            for h in range(8):
                for g in range(8):
                    i, j = 2 * h + il, 2 * g + jl
                    if i == 8 or j == 8:
                        continue
                    ni, nj = (16 - i) % 16, (16 - j) % 16
                    assert ni % 2 == il and nj % 2 == jl
                    for a in range(2):
                        out[2 * il + jl, g, h, a, nj // 2, ni // 2, a] = 1.0 - 2.0 * a
    return out.reshape(4, 128, 128)


def dotf(a, b):
    return jnp.dot(a, b, preferred_element_type=F32)


def dott(a, b):
    return lax.dot_general(a, b, (((1,), (1,)), ((), ())), preferred_element_type=F32)


def split(values):
    upper = values.astype(BF16)
    return upper, (values - upper.astype(F32)).astype(BF16)


def spectral_kernel(
    latent_ref, skip_ref, weight_ref, third_ref, back_ref, second_ref, first_ref, firstt_ref, pair_ref,
    out_ref,
    r1, z_msg, r2, s_msg, r3, t_msg, r4, mixing, n_msg, r5, g_msg, r6, f_msg, v_msg, r7, rv, b_msg, r8, skip,
    send, recv,
):
    me_x = lax.axis_index("gx")
    me_y = lax.axis_index("gy")
    me_z = lax.axis_index("gz")
    mine = {"gx": me_x, "gy": me_y, "gz": me_z}
    sizes = {"gx": GX, "gy": GY, "gz": GZ}

    barrier = pltpu.get_barrier_semaphore()
    total = 0
    for axis in ("gz", "gy", "gx"):
        for o in range(1, sizes[axis]):
            pl.semaphore_signal(
                barrier, inc=1, device_id={axis: lax.rem(mine[axis] + o, sizes[axis])}, device_id_type=MESH
            )
            total += 1
    pl.semaphore_wait(barrier, total)

    def start(stage, axis, source, target):
        copies = []
        size = sizes[axis]
        for o in range(1, size):
            peer = lax.rem(mine[axis] + o, size)
            copy = pltpu.make_async_remote_copy(
                src_ref=source(peer),
                dst_ref=target.at[mine[axis]],
                send_sem=send.at[stage, o],
                recv_sem=recv.at[stage, o],
                device_id={axis: peer},
                device_id_type=MESH,
            )
            copy.start()
            copies.append(copy)
        return copies

    def finish(copies):
        for copy in copies:
            copy.wait_recv()

    waiting = []

    first = start(0, "gz", lambda p: latent_ref.at[p], r1)
    waiting += first
    r1[me_z] = latent_ref[me_z]
    for z in range(8):
        here = latent_ref[:, 8 * z : 8 * z + 8, :].reshape(64, 128)
        skip[z] = dotf(skip_ref[...], here)
    for s in range(8):
        halves_of = []
        for b in range(2):
            halves_of.append(weight_ref[b, :, 8 * s : 8 * s + 8, :].astype(F32).reshape(128, 64))
        mixing[128 * s : 128 * s + 128, :] = jnp.concatenate(halves_of, axis=1).astype(BF16)
    finish(first)
    values = r1[...].reshape(512, 128)
    spectrum = dotf(third_ref[0], values) + dotf(third_ref[1], values)
    z_msg[...] = spectrum.astype(BF16).reshape(4, 64, 128)

    second = start(1, "gy", lambda p: z_msg.at[p], r2)
    waiting += second
    r2[me_y] = z_msg[me_y]
    finish(second)
    wide = jnp.concatenate(
        [r2[e, 32 * b : 32 * b + 32, :] for e in range(4) for b in range(2)], axis=1
    )
    rows = jnp.concatenate(
        [dott(second_ref[0, l], wide) + dott(second_ref[1, l], wide) for l in range(2)], axis=1
    )
    upper, lower = split(rows)
    partial = jnp.concatenate(
        [
            dotf(first_ref[0, l], upper) + dotf(first_ref[0, l], lower) + dotf(first_ref[1, l], upper)
            for l in range(2)
        ],
        axis=1,
    )
    s_msg[...] = partial.astype(BF16).reshape(8, 16, 128)

    third = start(2, "gx", lambda p: s_msg.at[p], r3)
    waiting += third
    r3[me_x] = s_msg[me_x]
    finish(third)
    modes = jnp.sum(r3[...].astype(F32), axis=0)
    for h in range(8):
        t_msg[h] = modes[2 * h : 2 * h + 2, :]

    fourth = start(3, "gz", lambda p: t_msg.at[p], r4)
    waiting += fourth
    r4[me_z] = t_msg[me_z]
    finish(fourth)
    mode_rows = lax.broadcasted_iota(jnp.int32, (16, 128), 0)
    lanes16 = lax.broadcasted_iota(jnp.int32, (16, 128), 1)
    own = mode_rows == lanes16 // 8
    expanded = jnp.concatenate(
        [
            jnp.concatenate(
                [
                    jnp.where(own, jnp.broadcast_to(r4[s, a : a + 1, :], (16, 128)), 0.0)
                    for s in range(8)
                ],
                axis=1,
            )
            for a in range(2)
        ],
        axis=0,
    ).astype(BF16)
    product = dotf(expanded, mixing[...])
    sign = jnp.where(lanes16 < 64, -1.0, 1.0)
    mixed = product[0:16] + pltpu.roll(product[16:32], 64, 1) * sign
    first_place = (me_x + me_y + me_z) == 0
    mixed = jnp.where((mode_rows == 0) & first_place, 0.0, mixed)
    spread = jnp.where(own, 1.0, 0.0).astype(BF16)
    tall = lax.dot_general(
        mixed.astype(BF16), spread, (((0,), (0,)), ((), ())), preferred_element_type=F32
    )
    tall_rows = lax.broadcasted_iota(jnp.int32, (128, 128), 0)
    tall_lanes = lax.broadcasted_iota(jnp.int32, (128, 128), 1)
    tall = jnp.where(tall_rows % 8 == tall_lanes % 8, tall, 0.0).astype(BF16)
    gather = (mode_rows % 2) * 8 + mode_rows // 2 == lanes16 // 8
    turned = dotf(jnp.where(gather, 1.0, 0.0).astype(BF16), tall)
    for h in range(8):
        n_msg[h] = turned[2 * h : 2 * h + 2, :]

    fifth = start(4, "gz", lambda p: n_msg.at[p], r5)
    waiting += fifth
    r5[me_z] = n_msg[me_z]
    finish(fifth)
    g_msg[...] = jnp.concatenate([r5[h] for h in range(8)], axis=0).astype(BF16)

    sixth = start(5, "gx", lambda p: g_msg, r6)
    waiting += sixth
    r6[me_x] = g_msg[...]
    finish(sixth)
    field = r6[...].reshape(128, 128)
    along = (
        dotf(firstt_ref[0, 0], field[:, 0:64])
        + dotf(firstt_ref[1, 0], field[:, 0:64])
        + dotf(firstt_ref[0, 1], field[:, 64:128])
        + dotf(firstt_ref[1, 1], field[:, 64:128])
    )
    upper, lower = split(along.T)
    plane = (
        dotf(upper[0:32], second_ref[0, 0])
        + dotf(lower[0:32], second_ref[0, 0])
        + dotf(upper[0:32], second_ref[1, 0])
        + dotf(upper[32:64], second_ref[0, 1])
        + dotf(lower[32:64], second_ref[0, 1])
        + dotf(upper[32:64], second_ref[1, 1])
    )
    zero_rows = lax.broadcasted_iota(jnp.int32, (32, 1024), 0)
    scale = 1.0 / GRID**3
    plane = plane * jnp.where((zero_rows < 8) & (me_y == 0), scale, 2.0 * scale)
    for e in range(4):
        for b in range(2):
            part = plane[:, (2 * e + b) * 128 : (2 * e + b + 1) * 128]
            f_msg[e, 32 * b : 32 * b + 32, :] = part.astype(BF16)

    seventh = start(6, "gy", lambda p: f_msg.at[p], r7)
    waiting += seventh
    r7[me_y] = f_msg[me_y]
    wide_field = field.astype(F32)
    lane_group = tall_lanes // 32
    paired = jnp.zeros((128, 128), F32)
    for p in range(4):
        paired = jnp.where(lane_group == p, dotf(pair_ref[p], field), paired)
    low = ((tall_lanes // 8) % 4 == 0) & (me_y == 0)
    power = jnp.where(low, 0.5 * wide_field * (wide_field + paired), 2.0 * wide_field * wide_field)
    power = jnp.sum(power, axis=0, keepdims=True)
    power = power + pltpu.roll(power, 64, 1)
    power = power + pltpu.roll(power, 32, 1)
    power = power + pltpu.roll(power, 16, 1)
    power = power + pltpu.roll(power, 8, 1)
    tall_power = jnp.broadcast_to(power, (128, 128)).T
    v_msg[...] = tall_power[0:8, :] * (scale * scale)
    eighth = start(7, "gy", lambda p: v_msg, rv)
    waiting += eighth
    rv[me_y] = v_msg[...]
    finish(seventh)
    grid_part = r7[...].reshape(256, 128)
    branch = dotf(back_ref[0], grid_part) + dotf(back_ref[1], grid_part)
    finish(eighth)
    variance = (rv[0] + rv[1]) + (rv[2] + rv[3])
    inverse = 1.0 / jnp.sqrt(variance + NORM_FLOOR)
    branch = branch.reshape(64, 8, 128) * inverse[None]
    b_msg[...] = branch.reshape(8, 64, 128).astype(BF16)

    ninth = start(8, "gz", lambda p: b_msg.at[p], r8)
    waiting += ninth
    r8[me_z] = b_msg[me_z]
    finish(ninth)
    for z in range(8):
        normed = r8[:, 8 * z : 8 * z + 8, :].astype(F32).reshape(64, 128)
        out_ref[:, z, :] = gelu(normed + skip[z]).T
    for copy in waiting:
        copy.wait_send()


def spectral_layer(latent, skip_t, weight, third, back, second, first, firstt, pair):
    vmem = pl.BlockSpec(memory_space=pltpu.VMEM)
    return pl.pallas_call(
        spectral_kernel,
        out_shape=jax.ShapeDtypeStruct((128, 8, 64), F32),
        in_specs=[vmem] * 9,
        out_specs=vmem,
        scratch_shapes=[
            pltpu.VMEM((8, 64, 128), BF16),
            pltpu.VMEM((4, 64, 128), BF16),
            pltpu.VMEM((4, 64, 128), BF16),
            pltpu.VMEM((8, 16, 128), BF16),
            pltpu.VMEM((8, 16, 128), BF16),
            pltpu.VMEM((8, 2, 128), F32),
            pltpu.VMEM((8, 2, 128), F32),
            pltpu.VMEM((1024, 128), BF16),
            pltpu.VMEM((8, 2, 128), F32),
            pltpu.VMEM((8, 2, 128), F32),
            pltpu.VMEM((16, 128), BF16),
            pltpu.VMEM((8, 16, 128), BF16),
            pltpu.VMEM((4, 64, 128), BF16),
            pltpu.VMEM((8, 128), F32),
            pltpu.VMEM((4, 64, 128), BF16),
            pltpu.VMEM((4, 8, 128), F32),
            pltpu.VMEM((8, 64, 128), BF16),
            pltpu.VMEM((8, 64, 128), BF16),
            pltpu.VMEM((8, 64, 128), F32),
            pltpu.SemaphoreType.DMA((9, 8)),
            pltpu.SemaphoreType.DMA((9, 8)),
        ],
        compiler_params=pltpu.CompilerParams(collective_id=0, has_side_effects=True),
    )(latent, skip_t, weight, third, back, second, first, firstt, pair)


def body(point_data, neighbours, counts, kernel_in, kernel_mid, kernel_out, spectral, skip_weight):
    count_y = lax.axis_size("gy")
    count_z = lax.axis_size("gz")
    place_x = lax.axis_index("gx")
    place_y = lax.axis_index("gy")
    place_z = lax.axis_index("gz")
    geometry_count, cells_x, cells_y, cells_z = neighbours.shape[0:4]
    per_device = point_data.shape[2]
    beside_all = extended(point_data[None, None, None], (("gx", 0), ("gy", 1), ("gz", 2)), 1)
    table = jnp.transpose(beside_all, (3, 4, 0, 1, 2, 5)).reshape(
        geometry_count, point_data.shape[1], 27, per_device
    )
    turned = jnp.transpose(neighbours[0], (3, 2, 0, 1)).reshape(NB, -1)
    owner = turned // per_device
    offset_z = owner % count_z - place_z + 1
    offset_y = owner // count_z % count_y - place_y + 1
    offset_x = owner // (count_z * count_y) - place_x + 1
    block_index = (offset_x * 3 + offset_y) * 3 + offset_z
    slot_index = turned % per_device
    centre_y = (
        (place_y * cells_y + jnp.arange(cells_y, dtype=jnp.int32)).astype(jnp.float32) + 0.5
    ) / GRID
    centre_z = (
        (place_z * cells_z + jnp.arange(cells_z, dtype=jnp.int32)).astype(jnp.float32) + 0.5
    ) / GRID
    centre_x = (
        (place_x * cells_x + jnp.arange(cells_x, dtype=jnp.int32)).astype(jnp.float32) + 0.5
    ) / GRID
    shape = (cells_z, cells_x, cells_y)
    centres = jnp.stack(
        [
            jnp.broadcast_to(centre_x[None, :, None], shape).reshape(-1),
            jnp.broadcast_to(centre_y[None, None, :], shape).reshape(-1),
            jnp.broadcast_to(centre_z[:, None, None], shape).reshape(-1),
        ]
    )
    centres = jnp.pad(centres, ((0, 5), (0, 0)))
    first = jnp.stack(
        [kernel_in[0], kernel_in[1], kernel_in[2], kernel_in[3], kernel_in[5]]
        + [jnp.zeros_like(kernel_in[0])] * 2
        + [kernel_in[4]],
        axis=1,
    )
    latent = encode(
        slot_index,
        block_index,
        jnp.transpose(counts[0], (2, 0, 1)).reshape(1, -1),
        centres,
        packed_table(table[0]),
        first,
        kernel_mid.T,
        kernel_out.T,
    )
    third = third_table()
    by_place = first_table()
    pick = lambda values: lax.dynamic_index_in_dim(jnp.asarray(halves(values)), place_x, 1, keepdims=False)
    out = spectral_layer(
        latent,
        skip_weight.T,
        spectral.reshape(2, 16, 64, 64),
        jnp.asarray(halves(third)),
        jnp.asarray(halves(third.T)),
        jnp.asarray(halves(second_table())),
        pick(by_place),
        pick(np.swapaxes(by_place, 2, 3)),
        jnp.asarray(pair_table().astype(ml_dtypes.bfloat16)),
    )
    return out.reshape(1, cells_x, cells_y, cells_z, -1)


def solution(mesh):
    in_specs = (
        P(None, None, ("gx", "gy", "gz")),
        P(None, "gx", "gy", "gz", None),
        P(None, "gx", "gy", "gz"),
        P(),
        P(),
        P(),
        P(None, "gz", "gx", "gy", None, None),
        P(),
    )
    out_specs = P(None, "gx", "gy", "gz", None)
    return jax.shard_map(body, mesh=mesh, in_specs=in_specs, out_specs=out_specs, check_vma=False)
```

time: 261 us -> 118 us (0.45)
  starting transfers between devices: 76.9 us -> 17.1 us
  Pallas kernels: 35.6 us -> 83.8 us
  waiting for transfers between devices: 51.1 us -> 3.92 us
  blocking collectives: 35.2 us -> 0 us
  local copies, waits for them, and re-layouts: 41.5 us -> 9.72 us
  matrix products: 8.9 us -> 0 us
  other arithmetic: 9.02 us -> 2.91 us
    all_to_all x13 -> x0, starting transfers between devices: 58 us -> none  [the longest x7 30.7 us: exchange(): lax.all_to_all(values.astype(jnp.bfloat16), axis, split_axis=split_axis,...]
    all_to_all x13 -> x0, waiting for transfers between devices: 49.7 us -> none  [the longest x7 28.2 us: exchange(): lax.all_to_all(values.astype(jnp.bfloat16), axis, split_axis=split_axis,...]
    pallas_call x0 -> x1, Pallas kernels: none -> 48.4 us  [spectral_layer(): pl.pallas_call(spectral_kernel, out_shape=jax.ShapeDtypeStruct((128, 8, 6...]
    all_to_all x4 -> x0, blocking collectives: 35.2 us -> none  [the longest x2 20.9 us: exchange(): lax.all_to_all(values.astype(jnp.bfloat16), axis, split_axis=split_axis,...]
    unnamed x36 -> x13, local copies, waits for them, and re-layouts: 15.1 us -> 4.61 us
    convert_element_type x10 -> x0, local copies, waits for them, and re-layouts: 9.16 us -> none  [the longest x7 4.95 us: exchange(): values.astype(jnp.bfloat16)]
    all_to_all x24 -> x0, local copies, waits for them, and re-layouts: 6.06 us -> none  [the longest x15 3.6 us: exchange(): lax.all_to_all(values.astype(jnp.bfloat16), axis, split_axis=split_axis,...]
    another operation x15 -> x3, local copies, waits for them, and re-layouts: 5.85 us -> 0.26 us  [body(): jnp.stack([jnp.broadcast_to(centre_x[None, :, None], shape).reshape(-1),...]
  transfers between devices with their start and end apart: 19 -> 6, of which waited for: 14 -> 1; matrix products, arithmetic and copies ran while one was open for 11% -> 7% of each run, Pallas kernels for 0% -> 0%
where the time goes in v1:
time: 118 us
  Pallas kernels  83.8 us (71%)
  starting transfers between devices  17.1 us (14%)
  local copies, waits for them, and re-layouts  9.72 us (8%)
  waiting for transfers between devices  3.92 us (3%)
  other arithmetic  2.91 us (2%)
    pallas_call x1, Pallas kernels, spectral_layer(): pl.pallas_call(spectral_kernel, out_shape=jax.ShapeDtypeStruct((128, 8, 6...  48.4 us
    pallas_call x1, Pallas kernels, encode(): pl.pallas_call(functools.partial(encoder_kernel, 27), grid=(nodes // widt...  35.4 us
    ppermute x3, starting transfers between devices, extended(): lax.ppermute(tail, axis, [(i, (i + 1) % count) for i in range(ends)])  12.6 us
    unnamed x13, local copies, waits for them, and re-layouts  4.61 us
    ppermute x3, starting transfers between devices, extended(): lax.ppermute(head, axis, [((i + 1) % count, i) for i in range(ends)])  4.5 us
    ppermute x3, waiting for transfers between devices, extended(): lax.ppermute(head, axis, [((i + 1) % count, i) for i in range(ends)])  3.91 us
  transfers between devices with their start and end apart: 6, of which 1 were waited for; matrix products, arithmetic and copies ran while one was open for 7% of the time, Pallas kernels for 0%

profile of v1, /device:TPU:1, one launch (start us, length us, event | category | flops | bytes accessed | tf_op | source)
XLA Modules:
  0.0 117.6 jit_solution(585067153862492496)
XLA Ops:
  0.0 4.3 %collective-permute-start = (f32[1,1,1,1,6,512]{5,0,4,3,2,1:T(1,128)}, f32[1,1,1,1,6,512]{5,0,4,3,2,1:T(1,128)S(1)}, u32[]{:S(2)}, u32[]{:S(2)}) collective-permute-start(f32[1,1,1,1,6,512]{5,0,4,3,2,1:T(1,128)} %bitcast.45), channel_id=1, source_target_pairs={{0,32},{32,64},{64,96},{96,128},{128,160},{160,192},{192,224},{1,3... | collective-permute-start | bytes 36872 | tf_op jit(solution)/shard_map/ppermute | solution.py:31
  4.4 1.3 %collective-permute-start.1 = (f32[1,1,1,1,6,512]{5,0,4,3,2,1:T(1,128)}, f32[1,1,1,1,6,512]{5,0,4,3,2,1:T(1,128)S(1)}, u32[]{:S(2)}, u32[]{:S(2)}) collective-permute-start(f32[1,1,1,1,6,512]{5,0,4,3,2,1:T(1,128)} %bitcast.46), channel_id=1, source_target_pairs={{32,0},{64,32},{96,64},{128,96},{160,128},{192,160},{224,192},{33,... | collective-permute-start | bytes 36872 | tf_op jit(solution)/shard_map/ppermute | solution.py:33
  5.7 0.7 copy-done.4
  6.4 1.1 copy.44
  7.5 0.2 copy.45
  7.7 1.1 fusion.10
  8.7 1.7 %dynamic-slice_bitcast_fusion = (bf16[2,2,128,128]{3,2,1,0:T(8,128)(2,1)}, bf16[2,2,128,128]{3,2,1,0:T(8,128)(2,1)}) fusion(bf16[2,8,2,128,128]{4,3,2,0,1:T(8,128)(2,1)} %constant.122.clone, s32[]{:T(128)S(6)} %select_n.37, bf16[2,8,2,128,128]{4,3,2,0,1:T(8,128)(2,1)} %constant.121.clone), kind=kLoop, calls=%fused_computation.38 | loop fusion | bytes 524292 | tf_op jit(solution)/shard_map/jit(dynamic_index_in_dim)/squeeze | solution.py:481
  10.5 3.2 %collective-permute-start.2 = (f32[3,1,1,1,6,512]{5,0,4,3,2,1:T(4,128)S(1)}, f32[3,1,1,1,6,512]{5,0,4,3,2,1:T(4,128)S(1)}, u32[]{:S(2)}, u32[]{:S(2)}) collective-permute-start(f32[3,1,1,1,6,512]{5,0,4,3,2,1:T(4,128)S(1)} %pad_maximum_fusion.1), channel_id=1, source_target_pairs={{0,8},{8,16},{16,24},{1,9},{9,17},{17,25},{2,10},{10,18},{18,26},{... | collective-permute-start | bytes 110600 | tf_op jit(solution)/shard_map/ppermute | solution.py:31
  13.7 1.3 %collective-permute-start.3 = (f32[3,1,1,1,6,512]{5,0,4,3,2,1:T(4,128)S(1)}, f32[3,1,1,1,6,512]{5,0,4,3,2,1:T(4,128)S(1)}, u32[]{:S(2)}, u32[]{:S(2)}) collective-permute-start(f32[3,1,1,1,6,512]{5,0,4,3,2,1:T(4,128)S(1)} %pad_maximum_fusion.1), channel_id=1, source_target_pairs={{8,0},{16,8},{24,16},{9,1},{17,9},{25,17},{10,2},{18,10},{26,18},{... | collective-permute-start | bytes 110600 | tf_op jit(solution)/shard_map/ppermute | solution.py:33
  15.1 0.7 copy.55.first_ref
  16.2 0.6 copy-done.1
  16.8 0.7 reshape.37.counts_ref
  17.6 0.7 copy.54
  18.3 0.7 copy.56
  19.0 5.0 %collective-permute-start.4 = (f32[3,3,1,1,6,512]{5,0,4,3,2,1:T(4,128)S(1)}, f32[3,3,1,1,6,512]{5,0,4,3,2,1:T(4,128)S(1)}, u32[]{:S(2)}, u32[]{:S(2)}) collective-permute-start(f32[3,3,1,1,6,512]{5,0,4,3,2,1:T(4,128)S(1)} %pad_maximum_fusion), channel_id=1, source_target_pairs={{0,1},{1,2},{2,3},{3,4},{4,5},{5,6},{6,7},{8,9},{9,10},{10,11},{11... | collective-permute-start | bytes 331784 | tf_op jit(solution)/shard_map/ppermute | solution.py:31
  24.0 1.9 %collective-permute-start.5 = (f32[3,3,1,1,6,512]{5,0,4,3,2,1:T(4,128)S(1)}, f32[3,3,1,1,6,512]{5,0,4,3,2,1:T(4,128)S(1)}, u32[]{:S(2)}, u32[]{:S(2)}) collective-permute-start(f32[3,3,1,1,6,512]{5,0,4,3,2,1:T(4,128)S(1)} %pad_maximum_fusion), channel_id=1, source_target_pairs={{1,0},{2,1},{3,2},{4,3},{5,4},{6,5},{7,6},{9,8},{10,9},{11,10},{12... | collective-permute-start | bytes 331784 | tf_op jit(solution)/shard_map/ppermute | solution.py:33
  26.0 0.6 select_maximum_fusion.centres_ref
  26.6 3.9 %collective-permute-done.5 = f32[3,3,1,1,6,512]{5,0,4,3,2,1:T(4,128)S(1)} collective-permute-done((f32[3,3,1,1,6,512]{5,0,4,3,2,1:T(4,128)S(1)}, f32[3,3,1,1,6,512]{5,0,4,3,2,1:T(4,128)S(1)}, u32[]{:S(2)}, u32[]{:S(2)}) %collective-permute-start.5) | collective-permute-done | bytes 110624 | tf_op jit(solution)/shard_map/ppermute | solution.py:33
  30.7 0.2 fusion.20
  31.1 0.1 copy.59
  31.2 0.7 fusion.2.table_ref
  31.9 35.4 %shard_map.136.latent_ref = bf16[8,64,128]{2,1,0:T(8,128)(2,1)} custom-call(s32[32,1024]{1,0:T(8,128)} %get-tuple-element.10.slots_ref, s32[32,1024]{1,0:T(8,128)} %get-tuple-element.9.blocks_ref, s32[1,1024]{1,0:T(1,128)} %reshape.37.counts_ref, f32[8,1024]{1,0:T(8,128)} %select_maximum_fusion.centres_ref, bf16[256,512]{1,0:T(8,128)(2,1)} %fusion.2.table_ref, ...), custom_call_target="tpu_custom_call" | custom-call | tf_op jit(solution)/shard_map/pallas_call | solution.py:98
  67.3 48.4 %shard_map.137 = f32[128,8,64]{2,1,0:T(8,128)} custom-call(bf16[8,64,128]{2,1,0:T(8,128)(2,1)} %shard_map.136.latent_ref, bf16[64,64]{1,0:T(8,128)(2,1)} %bitcast.51, bf16[2,16,64,64]{3,2,1,0:T(8,128)(2,1)} %bitcast.43, bf16[2,256,512]{2,1,0:T(8,128)(2,1)} %constant.118.clone.third_ref, bf16[2,512,256]{2,1,0:T(8,128)(2,1)} %constant.119.clone.back_ref, ...), custom_call_target="tpu_custom_call" | custom-call | tf_op jit(solution)/shard_map/pallas_call | solution.py:394
  115.7 1.9 %copy.61 = f32[1,8,16,8,64]{4,3,2,1,0:T(8,128)} copy(f32[1,8,16,8,64]{4,3,2,1,0:T(8,128)} %bitcast.39) | data formatting | bytes 524288
  (34 shorter events, 1.0 us)
Async XLA Ops:
  0.0 10.5 %collective-permute-start = (f32[1,1,1,1,6,512]{5,0,4,3,2,1:T(1,128)}, f32[1,1,1,1,6,512]{5,0,4,3,2,1:T(1,128)S(1)}, u32[]{:S(2)}, u32[]{:S(2)}) collective-permute-start(f32[1,1,1,1,6,512]{5,0,4,3,2,1:T(1,128)} %bitcast.45), channel_id=1, source_target_pairs={{0,32},{32,64},{64,96},{96,128},{128,160},{160,192},{192,224},{1,3... | collective-permute-start | bytes 36872 | tf_op jit(solution)/shard_map/ppermute | solution.py:31
  4.4 6.1 %collective-permute-start.1 = (f32[1,1,1,1,6,512]{5,0,4,3,2,1:T(1,128)}, f32[1,1,1,1,6,512]{5,0,4,3,2,1:T(1,128)S(1)}, u32[]{:S(2)}, u32[]{:S(2)}) collective-permute-start(f32[1,1,1,1,6,512]{5,0,4,3,2,1:T(1,128)} %bitcast.46), channel_id=1, source_target_pairs={{32,0},{64,32},{96,64},{128,96},{160,128},{192,160},{224,192},{33,... | collective-permute-start | bytes 36872 | tf_op jit(solution)/shard_map/ppermute | solution.py:33
  5.7 0.7 copy-start.4
  8.7 1.7 %copy-start = (f32[1,6,512]{2,0,1:T(1,128)S(1)}, f32[1,6,512]{2,0,1:T(1,128)}, u32[]{:S(2)}) copy-start(f32[1,6,512]{2,0,1:T(1,128)} %param.14) | copy-start | bytes 36868
  10.5 8.4 %collective-permute-start.2 = (f32[3,1,1,1,6,512]{5,0,4,3,2,1:T(4,128)S(1)}, f32[3,1,1,1,6,512]{5,0,4,3,2,1:T(4,128)S(1)}, u32[]{:S(2)}, u32[]{:S(2)}) collective-permute-start(f32[3,1,1,1,6,512]{5,0,4,3,2,1:T(4,128)S(1)} %pad_maximum_fusion.1), channel_id=1, source_target_pairs={{0,8},{8,16},{16,24},{1,9},{9,17},{17,25},{2,10},{10,18},{18,26},{... | collective-permute-start | bytes 110600 | tf_op jit(solution)/shard_map/ppermute | solution.py:31
  13.7 5.2 %collective-permute-start.3 = (f32[3,1,1,1,6,512]{5,0,4,3,2,1:T(4,128)S(1)}, f32[3,1,1,1,6,512]{5,0,4,3,2,1:T(4,128)S(1)}, u32[]{:S(2)}, u32[]{:S(2)}) collective-permute-start(f32[3,1,1,1,6,512]{5,0,4,3,2,1:T(4,128)S(1)} %pad_maximum_fusion.1), channel_id=1, source_target_pairs={{8,0},{16,8},{24,16},{9,1},{17,9},{25,17},{10,2},{18,10},{26,18},{... | collective-permute-start | bytes 110600 | tf_op jit(solution)/shard_map/ppermute | solution.py:33
  16.1 0.8 copy-start.1
  16.8 0.7 copy-start.2
  17.6 0.7 copy-start.3
  19.0 7.6 %collective-permute-start.4 = (f32[3,3,1,1,6,512]{5,0,4,3,2,1:T(4,128)S(1)}, f32[3,3,1,1,6,512]{5,0,4,3,2,1:T(4,128)S(1)}, u32[]{:S(2)}, u32[]{:S(2)}) collective-permute-start(f32[3,3,1,1,6,512]{5,0,4,3,2,1:T(4,128)S(1)} %pad_maximum_fusion), channel_id=1, source_target_pairs={{0,1},{1,2},{2,3},{3,4},{4,5},{5,6},{6,7},{8,9},{9,10},{10,11},{11... | collective-permute-start | bytes 331784 | tf_op jit(solution)/shard_map/ppermute | solution.py:31
  24.0 6.5 %collective-permute-start.5 = (f32[3,3,1,1,6,512]{5,0,4,3,2,1:T(4,128)S(1)}, f32[3,3,1,1,6,512]{5,0,4,3,2,1:T(4,128)S(1)}, u32[]{:S(2)}, u32[]{:S(2)}) collective-permute-start(f32[3,3,1,1,6,512]{5,0,4,3,2,1:T(4,128)S(1)} %pad_maximum_fusion), channel_id=1, source_target_pairs={{1,0},{2,1},{3,2},{4,3},{5,4},{6,5},{7,6},{9,8},{10,9},{11,10},{12... | collective-permute-start | bytes 331784 | tf_op jit(solution)/shard_map/ppermute | solution.py:33

commit v2 on v1

--- a/solution.py
+++ b/solution.py
@@ -20,98 +20,222 @@
 MESH = pl.DeviceIdType.MESH
 
 
-def extended(cells, sides, width):
-    for axis, dim in sides:
-        count = lax.axis_size(axis)
-        ends = count - 1
-        head = lax.slice_in_dim(cells, 0, width, axis=dim)
-        tail = lax.slice_in_dim(cells, cells.shape[dim] - width, cells.shape[dim], axis=dim)
-        cells = jnp.concatenate(
-            [
-                lax.ppermute(tail, axis, [(i, (i + 1) % count) for i in range(ends)]),
-                cells,
-                lax.ppermute(head, axis, [((i + 1) % count, i) for i in range(ends)]),
-            ],
-            axis=dim,
-        )
-    return cells
-
-
 def gelu(v):
     inner = v * (0.7978845608028654 + 0.035677408136300125 * (v * v))
     half = 0.5 * v
     return half + half * jnp.tanh(inner)
 
 
+def twice_gelu(v):
+    return v + v * jnp.tanh(v * (0.7978845608028654 + 0.035677408136300125 * (v * v)))
+
+
+SLOTS = 4
+ROWS = 256
+OFFSETS = [(dx, dy, dz) for dx in (-1, 0, 1) for dy in (-1, 0, 1) for dz in (-1, 0, 1)]
+
+
+def halo_kernel(
+    points_ref, near_ref, counts_ref, table_ref, slots_ref, blocks_ref, info_ref, rank_ref,
+    main, rest, send, recv,
+):
+    me_x = lax.axis_index("gx")
+    me_y = lax.axis_index("gy")
+    me_z = lax.axis_index("gz")
+
+    def device(offset):
+        dx, dy, dz = offset
+        return {
+            "gx": lax.rem(me_x + dx + GX, GX),
+            "gy": lax.rem(me_y + dy + GY, GY),
+            "gz": lax.rem(me_z + dz + GZ, GZ),
+        }
+
+    barrier = pltpu.get_barrier_semaphore()
+    peers = [o for o in OFFSETS if o != (0, 0, 0)]
+    for offset in peers:
+        pl.semaphore_signal(barrier, inc=1, device_id=device(offset), device_id_type=MESH)
+
+    points = points_ref[...]
+    upper = points.astype(BF16).astype(F32)
+    lower = points - upper
+    main[13] = jnp.concatenate([upper[0:4], lower[0:3], upper[4:5]], axis=0).astype(BF16)
+    rest[13] = upper[5:6]
+    pl.semaphore_wait(barrier, len(peers))
+    copies = []
+    for n, offset in enumerate(peers):
+        slot = 26 - OFFSETS.index(offset)
+        for k, buffer in enumerate((main, rest)):
+            copy = pltpu.make_async_remote_copy(
+                src_ref=buffer.at[13],
+                dst_ref=buffer.at[slot],
+                send_sem=send.at[k, n],
+                recv_sem=recv.at[k, n],
+                device_id=device(offset),
+                device_id_type=MESH,
+            )
+            copy.start()
+            copies.append(copy)
+
+    lane = lax.broadcasted_iota(jnp.int32, (1, 1024), 1)
+    counts = counts_ref[...].astype(F32)
+    key = counts * 1024.0 + (1023 - lane).astype(F32)
+    ones = jnp.ones((8, 128), BF16)
+    rank = jnp.zeros((8, 1024), F32)
+    for m in range(8):
+        tall = jnp.broadcast_to(key[:, 128 * m : 128 * m + 128], (128, 128)).T
+        ahead = jnp.concatenate(
+            [
+                jnp.where(tall > key[:, 128 * n : 128 * n + 128], 1.0, 0.0).astype(BF16)
+                for n in range(8)
+            ],
+            axis=1,
+        )
+        rank = rank + jnp.dot(ones, ahead, preferred_element_type=F32)
+    rank_ref[...] = rank
+    near = jnp.concatenate(
+        [near_ref[pl.ds(z, 128, stride=8), :].astype(F32).T for z in range(8)], axis=1
+    ).astype(jnp.int32)
+    owner = near >> 9
+    part = near & 511
+    block = ((((owner >> 5) - me_x + 1) * 3) + ((owner >> 3) & 3) - me_y + 1) * 3 + (owner & 7) - me_z + 1
+    code = jnp.clip(block, 0, 26) * 2 + (part >> 8)
+    place_y = (me_y * 16 + (lane & 15)).astype(F32)
+    place_x = (me_x * 8 + ((lane >> 4) & 7)).astype(F32)
+    place_z = (me_z * 8 + (lane >> 7)).astype(F32)
+    centres = [-(place + 0.5) / GRID for place in (place_x, place_y, place_z)]
+    rows = jnp.concatenate(
+        [(part & 255).astype(F32), code.astype(F32), counts] + centres + [jnp.zeros((12, 1024), F32)], axis=0
+    ).astype(BF16)
+    order = lax.broadcasted_iota(jnp.int32, (128, 1024), 0).astype(F32)
+    wide_rank = rank[0:1]
+    for t in range(8):
+        moved = jnp.where(order + 128.0 * t == wide_rank, 1.0, 0.0).astype(BF16)
+        moved = lax.dot_general(rows, moved, (((1,), (1,)), ((), ())), preferred_element_type=F32)
+        code = moved[32:64].astype(jnp.int32)
+        slots_ref[t] = moved[0:32].astype(jnp.int32) + 256 * (code & 1)
+        blocks_ref[t] = code >> 1
+        info_ref[t] = moved[64:72]
+
+    for copy in copies:
+        copy.wait_recv()
+    table_ref[0:216, :] = main[...].astype(F32).reshape(216, 512).astype(BF16)
+    tail = jnp.concatenate([rest[b] for b in range(27)] + [jnp.zeros((13, 512), F32)], axis=0)
+    table_ref[216:256, :] = tail.astype(BF16)
+    for copy in copies:
+        copy.wait_send()
+
+
+def halo(points, near, counts):
+    vmem = pl.BlockSpec(memory_space=pltpu.VMEM)
+    return pl.pallas_call(
+        halo_kernel,
+        out_shape=[
+            jax.ShapeDtypeStruct((ROWS, 512), BF16),
+            jax.ShapeDtypeStruct((8, NB, 128), jnp.int32),
+            jax.ShapeDtypeStruct((8, NB, 128), jnp.int32),
+            jax.ShapeDtypeStruct((8, 8, 128), F32),
+            jax.ShapeDtypeStruct((8, 1024), F32),
+        ],
+        in_specs=[vmem] * 3,
+        out_specs=[vmem] * 5,
+        scratch_shapes=[
+            pltpu.VMEM((27, 8, 512), BF16),
+            pltpu.VMEM((27, 1, 512), F32),
+            pltpu.SemaphoreType.DMA((2, 26)),
+            pltpu.SemaphoreType.DMA((2, 26)),
+        ],
+        compiler_params=pltpu.CompilerParams(collective_id=1, has_side_effects=True),
+    )(points, near, counts)
+
+
 def encoder_kernel(
-    blocks, slots_ref, blocks_ref, counts_ref, centres_ref, table_ref, first_ref, mid_ref, last_ref, out_ref, total
+    table_ref, slots_ref, blocks_ref, info_ref, rank_ref, in_ref, mid_ref, last_ref, out_ref,
+    first_scr, mid_scr, last_scr, ordered,
 ):
-    width = slots_ref.shape[1]
-    per_device = table_ref.shape[1]
-    rest_rows = table_ref.shape[0] - 8 * blocks
-    slot_ids = lax.broadcasted_iota(jnp.int32, (per_device, width), 0).astype(jnp.int16)
-    rest_ids = lax.broadcasted_iota(jnp.int32, (rest_rows, width), 0)
-    rows = lax.broadcasted_iota(jnp.int32, (8, width), 0)
-    counts = counts_ref[...]
-    centres = centres_ref[...]
-    total[...] = jnp.zeros_like(total)
-
-    def step(s, carry):
-        slot = jnp.broadcast_to(slots_ref[pl.ds(s, 1), :], (16, width)).astype(jnp.int16)
-        slot = jnp.concatenate([slot] * (per_device // 16), axis=0)
-        hot = jnp.where(slot_ids == slot, jnp.bfloat16(1), jnp.bfloat16(0))
-        found = jnp.dot(table_ref[...], hot, preferred_element_type=jnp.float32)
-        block = blocks_ref[pl.ds(s, 1), :]
-        wide = jnp.broadcast_to(block, (8, width))
-        picked = found[0:8]
-        for b in range(1, blocks):
-            picked = jnp.where(wide == b, found[8 * b : 8 * b + 8], picked)
-        third = jnp.sum(jnp.where(rest_ids == block, found[8 * blocks :], 0.0), axis=0, keepdims=True)
-        place = picked + pltpu.roll(picked, 4, 0) - centres
-        pair = jnp.where(rows < 3, place, jnp.where(rows == 4, third, picked)).astype(jnp.bfloat16)
-        hidden = gelu(jnp.dot(first_ref[...], pair, preferred_element_type=jnp.float32))
-        hidden = gelu(
-            jnp.dot(mid_ref[...], hidden.astype(jnp.bfloat16), preferred_element_type=jnp.float32)
+    column = lax.broadcasted_iota(jnp.int32, (6, ROWS), 1)
+    feature = lax.broadcasted_iota(jnp.int32, (6, ROWS), 0)
+    value = column % 8
+    wanted = jnp.where(value < 4, value, jnp.where(value == 7, 4, value - 4))
+    wanted = jnp.where(column >= 243, column - 243, jnp.where(column >= 216, 5, wanted))
+    chosen = jnp.where((feature == wanted) & (column < 246), 1.0, 0.0).astype(BF16)
+    turn = (((0,), (0,)), ((), ()))
+    first_scr[...] = lax.dot_general(in_ref[...], chosen, turn, preferred_element_type=F32).astype(BF16)
+    mid_scr[...] = (mid_ref[...].astype(F32).T * 0.5).astype(BF16)
+    last_scr[...] = last_ref[...].astype(F32).T.astype(BF16)
+
+    slot_ids = lax.broadcasted_iota(jnp.int32, (512, 128), 0).astype(jnp.int16)
+    row = lax.broadcasted_iota(jnp.int32, (ROWS, 128), 0)
+    row_block = jnp.where(row < 216, row // 8, jnp.where(row < 243, row - 216, -1)).astype(jnp.int16)
+    zero = jnp.zeros((240, 128), BF16)
+    last_rows = lax.broadcasted_iota(jnp.int32, (16, 128), 0)
+
+    def chunk(c, carry):
+        lanes = pl.ds(pl.multiple_of(c * 128, 128), 128)
+        info = info_ref[c]
+        counts = info[0:1]
+        most = jnp.max(counts).astype(jnp.int32)
+        centre = jnp.zeros((16, 128), F32)
+        for d in range(3):
+            centre = jnp.where(last_rows == 3 + d, info[1 + d : 2 + d], centre)
+        base = jnp.concatenate([zero, centre.astype(BF16)], axis=0)
+
+        def step(t, total):
+            hot = []
+            for u in range(SLOTS):
+                slot = jnp.broadcast_to(slots_ref[c, pl.ds(SLOTS * t + u, 1), :], (16, 128)).astype(jnp.int16)
+                slot = jnp.concatenate([slot] * 32, axis=0)
+                hot.append(jnp.where(slot_ids == slot, BF16(1), BF16(0)))
+            found = jnp.dot(table_ref[...], jnp.concatenate(hot, axis=1), preferred_element_type=F32)
+            found = found.astype(BF16)
+            kept = []
+            for u in range(SLOTS):
+                block = jnp.broadcast_to(blocks_ref[c, pl.ds(SLOTS * t + u, 1), :], (16, 128)).astype(jnp.int16)
+                block = jnp.concatenate([block] * (ROWS // 16), axis=0)
+                kept.append(jnp.where(row_block == block, found[:, 128 * u : 128 * u + 128], base))
+            hidden = jnp.dot(first_scr[...], jnp.concatenate(kept, axis=1), preferred_element_type=F32)
+            hidden = twice_gelu(hidden).astype(BF16)
+            hidden = twice_gelu(jnp.dot(mid_scr[...], hidden, preferred_element_type=F32))
+            for u in range(SLOTS):
+                used = (SLOTS * t + u).astype(F32) < counts
+                total = total + jnp.where(used, hidden[:, 128 * u : 128 * u + 128], 0.0)
+            return total
+
+        total = lax.fori_loop(0, (most + SLOTS - 1) // SLOTS, step, jnp.zeros((80, 128), F32))
+        mean = total * (0.5 / counts)
+        upper = mean.astype(BF16)
+        lower = (mean - upper.astype(F32)).astype(BF16)
+        last = last_scr[...]
+        values = jnp.dot(last, upper, preferred_element_type=F32) + jnp.dot(
+            last, lower, preferred_element_type=F32
         )
-        hidden = hidden.astype(jnp.bfloat16).astype(jnp.float32)
-        total[...] += jnp.where(s < counts, hidden, 0.0)
+        ordered[:, lanes] = values.astype(BF16)
         return carry
 
-    lax.fori_loop(0, slots_ref.shape[0], step, 0, unroll=8)
-    mean = total[...] / counts.astype(jnp.float32)
-    upper = mean.astype(jnp.bfloat16)
-    lower = (mean - upper.astype(jnp.float32)).astype(jnp.bfloat16)
-    last = last_ref[...]
-    values = jnp.dot(last, upper, preferred_element_type=jnp.float32) + jnp.dot(
-        last, lower, preferred_element_type=jnp.float32
-    )
-    tiles = width // 128
-    parts = [values[:, 128 * t : 128 * t + 128].reshape(8, 8, 128) for t in range(tiles)]
-    out_ref[...] = jnp.stack(parts, axis=1).reshape(8, 8 * tiles, 128).astype(jnp.bfloat16)
-
-
-def encode(slots, block_ids, counts, centres, table, first, mid, last):
-    nodes = slots.shape[1]
-    width = min(512, nodes)
-    tile = lambda rows: pl.BlockSpec((rows, width), lambda i: (0, i))
-    whole = lambda array: pl.BlockSpec(array.shape, lambda i: (0, 0))
+    lax.fori_loop(0, 8, chunk, 0)
+    order = lax.broadcasted_iota(jnp.int32, (1024, 128), 0).astype(F32)
+    parts = []
+    for t in range(8):
+        moved = jnp.where(order == rank_ref[0:1, 128 * t : 128 * t + 128], 1.0, 0.0).astype(BF16)
+        part = jnp.dot(ordered[...], moved, preferred_element_type=F32)
+        parts.append(part.reshape(8, 8, 128))
+    out_ref[...] = jnp.stack(parts, axis=1).reshape(8, 64, 128).astype(BF16)
+
+
+def encode(table, slots, blocks, info, rank, kernel_in, kernel_mid, kernel_out):
+    vmem = pl.BlockSpec(memory_space=pltpu.VMEM)
     return pl.pallas_call(
-        functools.partial(encoder_kernel, 27),
-        grid=(nodes // width,),
-        out_shape=jax.ShapeDtypeStruct((8, nodes // 16, 128), jnp.bfloat16),
-        in_specs=[tile(NB), tile(NB), tile(1), tile(8), whole(table), whole(first), whole(mid), whole(last)],
-        out_specs=pl.BlockSpec((8, width // 16, 128), lambda i: (0, i, 0)),
-        scratch_shapes=[pltpu.VMEM((mid.shape[0], width), jnp.float32)],
-    )(slots, block_ids, counts, centres, table, first, mid, last)
-
-
-def packed_table(table):
-    upper = table.astype(jnp.bfloat16)
-    lower = (table - upper.astype(jnp.float32)).astype(jnp.bfloat16)
-    main = jnp.concatenate([upper[0:3], upper[3:4], lower[0:3], upper[4:5]], axis=0)
-    main = jnp.transpose(main, (1, 0, 2)).reshape(-1, table.shape[2])
-    rows = jnp.concatenate([main, upper[5]], axis=0)
-    return jnp.pad(rows, ((0, -rows.shape[0] % 128), (0, 0)))
+        encoder_kernel,
+        out_shape=jax.ShapeDtypeStruct((8, 64, 128), BF16),
+        in_specs=[vmem] * 8,
+        out_specs=vmem,
+        scratch_shapes=[
+            pltpu.VMEM((80, ROWS), BF16),
+            pltpu.VMEM((80, 80), BF16),
+            pltpu.VMEM((64, 80), BF16),
+            pltpu.VMEM((64, 1024), BF16),
+        ],
+    )(table, slots, blocks, info, rank, kernel_in, kernel_mid, kernel_out)
 
 
 def halves(values):
@@ -155,8 +279,11 @@
     i = np.arange(16)
     cos, sin = turn(centred(i)[:, None], np.arange(64)[None, :])
     both = complex_block(cos, sin).reshape(8, 2, 8, 8, 2, 2)
-    full = np.einsum("hltxab,gf->tlghafbx", both, np.eye(8))
-    return full.reshape(8, 2, 128, 128)
+    return np.einsum("hltxab->tlhabx", both).reshape(8, 2, 16, 16)
+
+
+def placed(values):
+    return np.tile(np.moveaxis(halves(values), 0, 1), (1, 1, 1, 1, 8))
 
 
 @functools.lru_cache(None)
@@ -210,6 +337,12 @@
             )
             total += 1
     pl.semaphore_wait(barrier, total)
+
+    same = lax.broadcasted_iota(jnp.int32, (128, 128), 0) // 16 == lax.broadcasted_iota(jnp.int32, (128, 128), 1) // 16
+
+    def spread_blocks(ref, part, l):
+        small = ref[me_x, part, l].astype(F32)
+        return jnp.where(same, jnp.concatenate([small] * 8, axis=0), 0.0).astype(BF16)
 
     def start(stage, axis, source, target):
         copies = []
@@ -237,9 +370,12 @@
     first = start(0, "gz", lambda p: latent_ref.at[p], r1)
     waiting += first
     r1[me_z] = latent_ref[me_z]
+    first_tab = [[spread_blocks(first_ref, p, l) for l in range(2)] for p in range(2)]
+    back_tab = [[spread_blocks(firstt_ref, p, l) for l in range(2)] for p in range(2)]
+    skip_t = skip_ref[...].astype(F32).T.astype(BF16)
     for z in range(8):
         here = latent_ref[:, 8 * z : 8 * z + 8, :].reshape(64, 128)
-        skip[z] = dotf(skip_ref[...], here)
+        skip[z] = dotf(skip_t, here)
     for s in range(8):
         halves_of = []
         for b in range(2):
@@ -263,7 +399,7 @@
     upper, lower = split(rows)
     partial = jnp.concatenate(
         [
-            dotf(first_ref[0, l], upper) + dotf(first_ref[0, l], lower) + dotf(first_ref[1, l], upper)
+            dotf(first_tab[0][l], upper) + dotf(first_tab[0][l], lower) + dotf(first_tab[1][l], upper)
             for l in range(2)
         ],
         axis=1,
@@ -327,10 +463,10 @@
     finish(sixth)
     field = r6[...].reshape(128, 128)
     along = (
-        dotf(firstt_ref[0, 0], field[:, 0:64])
-        + dotf(firstt_ref[1, 0], field[:, 0:64])
-        + dotf(firstt_ref[0, 1], field[:, 64:128])
-        + dotf(firstt_ref[1, 1], field[:, 64:128])
+        dotf(back_tab[0][0], field[:, 0:64])
+        + dotf(back_tab[1][0], field[:, 0:64])
+        + dotf(back_tab[0][1], field[:, 64:128])
+        + dotf(back_tab[1][1], field[:, 64:128])
     )
     upper, lower = split(along.T)
     plane = (
@@ -424,70 +560,24 @@
 
 
 def body(point_data, neighbours, counts, kernel_in, kernel_mid, kernel_out, spectral, skip_weight):
-    count_y = lax.axis_size("gy")
-    count_z = lax.axis_size("gz")
-    place_x = lax.axis_index("gx")
-    place_y = lax.axis_index("gy")
-    place_z = lax.axis_index("gz")
-    geometry_count, cells_x, cells_y, cells_z = neighbours.shape[0:4]
-    per_device = point_data.shape[2]
-    beside_all = extended(point_data[None, None, None], (("gx", 0), ("gy", 1), ("gz", 2)), 1)
-    table = jnp.transpose(beside_all, (3, 4, 0, 1, 2, 5)).reshape(
-        geometry_count, point_data.shape[1], 27, per_device
-    )
-    turned = jnp.transpose(neighbours[0], (3, 2, 0, 1)).reshape(NB, -1)
-    owner = turned // per_device
-    offset_z = owner % count_z - place_z + 1
-    offset_y = owner // count_z % count_y - place_y + 1
-    offset_x = owner // (count_z * count_y) - place_x + 1
-    block_index = (offset_x * 3 + offset_y) * 3 + offset_z
-    slot_index = turned % per_device
-    centre_y = (
-        (place_y * cells_y + jnp.arange(cells_y, dtype=jnp.int32)).astype(jnp.float32) + 0.5
-    ) / GRID
-    centre_z = (
-        (place_z * cells_z + jnp.arange(cells_z, dtype=jnp.int32)).astype(jnp.float32) + 0.5
-    ) / GRID
-    centre_x = (
-        (place_x * cells_x + jnp.arange(cells_x, dtype=jnp.int32)).astype(jnp.float32) + 0.5
-    ) / GRID
-    shape = (cells_z, cells_x, cells_y)
-    centres = jnp.stack(
-        [
-            jnp.broadcast_to(centre_x[None, :, None], shape).reshape(-1),
-            jnp.broadcast_to(centre_y[None, None, :], shape).reshape(-1),
-            jnp.broadcast_to(centre_z[:, None, None], shape).reshape(-1),
-        ]
-    )
-    centres = jnp.pad(centres, ((0, 5), (0, 0)))
-    first = jnp.stack(
-        [kernel_in[0], kernel_in[1], kernel_in[2], kernel_in[3], kernel_in[5]]
-        + [jnp.zeros_like(kernel_in[0])] * 2
-        + [kernel_in[4]],
-        axis=1,
-    )
-    latent = encode(
-        slot_index,
-        block_index,
+    cells_x, cells_y, cells_z = neighbours.shape[1:4]
+    made = halo(
+        point_data[0],
+        neighbours.reshape(-1, NB),
         jnp.transpose(counts[0], (2, 0, 1)).reshape(1, -1),
-        centres,
-        packed_table(table[0]),
-        first,
-        kernel_mid.T,
-        kernel_out.T,
-    )
+    )
+    latent = encode(*made, kernel_in, kernel_mid, kernel_out)
     third = third_table()
     by_place = first_table()
-    pick = lambda values: lax.dynamic_index_in_dim(jnp.asarray(halves(values)), place_x, 1, keepdims=False)
     out = spectral_layer(
         latent,
-        skip_weight.T,
+        skip_weight,
         spectral.reshape(2, 16, 64, 64),
         jnp.asarray(halves(third)),
         jnp.asarray(halves(third.T)),
         jnp.asarray(halves(second_table())),
-        pick(by_place),
-        pick(np.swapaxes(by_place, 2, 3)),
+        jnp.asarray(placed(by_place)),
+        jnp.asarray(placed(np.swapaxes(by_place, 2, 3))),
         jnp.asarray(pair_table().astype(ml_dtypes.bfloat16)),
     )
     return out.reshape(1, cells_x, cells_y, cells_z, -1)

time: 118 us -> 98 us (0.83)
  starting transfers between devices: 17.1 us -> 0 us
  Pallas kernels: 83.8 us -> 93.2 us
  local copies, waits for them, and re-layouts: 9.72 us -> 4.58 us
  waiting for transfers between devices: 3.92 us -> 0 us
  other arithmetic: 2.91 us -> 0 us
    ppermute x6 -> x0, starting transfers between devices: 17.1 us -> none  [the longest x3 12.6 us: extended(): lax.ppermute(tail, axis, [(i, (i + 1) % count) for i in range(ends)])]
    pallas_call x1 -> x2, Pallas kernels: 35.4 us -> 49.6 us  [the longest x1 31.8 us: encode(): pl.pallas_call(encoder_kernel, out_shape=jax.ShapeDtypeStruct((8, 64, 128...]
    pallas_call x1, Pallas kernels: 48.4 us -> 43.6 us  [spectral_layer(): pl.pallas_call(spectral_kernel, out_shape=jax.ShapeDtypeStruct((128, 8, 6...]
    ppermute x6 -> x0, waiting for transfers between devices: 3.92 us -> none  [the longest x3 3.91 us: extended(): lax.ppermute(head, axis, [((i + 1) % count, i) for i in range(ends)])]
    squeeze x1 -> x0, local copies, waits for them, and re-layouts: 1.71 us -> none  [body(): lax.dynamic_index_in_dim(jnp.asarray(halves(values)), place_x, 1, keepdim...]
    transpose x3 -> x0, local copies, waits for them, and re-layouts: 1.39 us -> none  [the longest x1 1.14 us: body(): turned = jnp.transpose(neighbours[0], (3, 2, 0, 1)).reshape(NB, -1)]
    unnamed x13 -> x7, local copies, waits for them, and re-layouts: 4.61 us -> 3.9 us
  transfers between devices with their start and end apart: 6 -> 0, of which waited for: 1 -> 0; matrix products, arithmetic and copies ran while one was open for 7% -> 0% of each run, Pallas kernels for 0% -> 0%
where the time goes in v2:
time: 98 us; the launch traced here: 97.8 us
  Pallas kernels  93.2 us (95%)
  local copies, waits for them, and re-layouts  4.58 us (5%)
    pallas_call x1, Pallas kernels, spectral_layer(): pl.pallas_call(spectral_kernel, out_shape=jax.ShapeDtypeStruct((128, 8, 6...  43.6 us
    pallas_call x1, Pallas kernels, encode(): pl.pallas_call(encoder_kernel, out_shape=jax.ShapeDtypeStruct((8, 64, 128...  31.8 us
    pallas_call x1, Pallas kernels, halo(): pl.pallas_call(halo_kernel, out_shape=[jax.ShapeDtypeStruct((ROWS, 512),...  17.8 us
    unnamed x7, local copies, waits for them, and re-layouts  3.9 us

profile of v2, /device:TPU:1, one launch (start us, length us, event | category | flops | bytes accessed | tf_op | source)
XLA Modules:
  0.0 97.8 jit_solution(18333890716288368448)
XLA Ops:
  0.0 0.0 copy-start.1
  0.0 0.0 copy-start
  0.0 1.3 %copy.19 = f32[1,6,512]{2,1,0:T(8,128)} copy(f32[1,6,512]{2,0,1:T(1,128)} %param.14) | data formatting | bytes 24576
  1.3 0.0 copy-done.1
  1.3 0.7 copy.16.last_ref
  2.0 0.0 copy-done
  2.0 0.7 reshape.13.counts_ref
  2.7 17.8 %shard_map.136 = (bf16[256,512]{1,0:T(8,128)(2,1)}, s32[8,32,128]{2,1,0:T(8,128)}, s32[8,32,128]{2,1,0:T(8,128)}, f32[8,8,128]{2,1,0:T(8,128)}, f32[8,1024]{1,0:T(8,128)}) custom-call(f32[6,512]{1,0:T(8,128)} %bitcast.12, s32[1024,32]{1,0:T(8,128)} %bitcast.11, s32[1,1024]{1,0:T(1,128)} %reshape.13.counts_ref), custom_call_target="tpu_custom_call" | custom-call | tf_op jit(solution)/shard_map/pallas_call | solution.py:131
  20.5 31.8 %shard_map.137.latent_ref = bf16[8,64,128]{2,1,0:T(8,128)(2,1)} custom-call(bf16[256,512]{1,0:T(8,128)(2,1)} %get-tuple-element.10.table_ref, s32[8,32,128]{2,1,0:T(8,128)} %get-tuple-element.11.slots_ref, s32[8,32,128]{2,1,0:T(8,128)} %get-tuple-element.12.blocks_ref, f32[8,8,128]{2,1,0:T(8,128)} %get-tuple-element.13.info_ref, ...), custom_call_target="tpu_custom_call" | custom-call | tf_op jit(solution)/shard_map/pallas_call | solution.py:227
  52.3 43.6 %shard_map.138 = f32[128,8,64]{2,1,0:T(8,128)} custom-call(bf16[8,64,128]{2,1,0:T(8,128)(2,1)} %shard_map.137.latent_ref, bf16[64,64]{1,0:T(8,128)(2,1)} %skip_ref.1, bf16[2,16,64,64]{3,2,1,0:T(8,128)(2,1)} %bitcast.10, bf16[2,256,512]{2,1,0:T(8,128)(2,1)} %constant.12.clone.third_ref, bf16[2,512,256]{2,1,0:T(8,128)(2,1)} %constant.13.clone.back_ref, ...), custom_call_target="tpu_custom_call" | custom-call | tf_op jit(solution)/shard_map/pallas_call | solution.py:530
  95.9 1.9 %copy.21 = f32[1,8,16,8,64]{4,3,2,1,0:T(8,128)} copy(f32[1,8,16,8,64]{4,3,2,1,0:T(8,128)} %bitcast.9) | data formatting | bytes 524288
  (1 shorter events, 0.0 us)
Async XLA Ops:
  0.0 1.3 %copy-start.1 = (bf16[80,64]{0,1:T(8,128)(2,1)S(1)}, bf16[80,64]{0,1:T(8,128)(2,1)}, u32[]{:S(2)}) copy-start(bf16[80,64]{0,1:T(8,128)(2,1)} %param.19) | copy-start | bytes 30724
  0.0 2.0 %copy-start = (s32[1,8,16,8]{2,3,1,0:T(8,128)S(1)}, s32[1,8,16,8]{2,3,1,0:T(8,128)}, u32[]{:S(2)}) copy-start(s32[1,8,16,8]{2,3,1,0:T(8,128)} %param.16) | copy-start | bytes 12292

commit v3 on v2

--- a/solution.py
+++ b/solution.py
@@ -27,17 +27,23 @@
 
 
 def twice_gelu(v):
-    return v + v * jnp.tanh(v * (0.7978845608028654 + 0.035677408136300125 * (v * v)))
+    if not GELU16:
+        return v + v * jnp.tanh(v * (0.7978845608028654 + 0.035677408136300125 * (v * v)))
+    v = v.astype(BF16)
+    inner = v * (BF16(0.7978845608028654) + BF16(0.035677408136300125) * (v * v))
+    return v + v * jnp.tanh(inner)
 
 
 SLOTS = 4
-ROWS = 256
+ROWS = 176
+FOUR, SIX = 108, 162
+GELU16 = True
 OFFSETS = [(dx, dy, dz) for dx in (-1, 0, 1) for dy in (-1, 0, 1) for dz in (-1, 0, 1)]
 
 
 def halo_kernel(
     points_ref, near_ref, counts_ref, table_ref, slots_ref, blocks_ref, info_ref, rank_ref,
-    main, rest, send, recv,
+    main, send, recv,
 ):
     me_x = lax.axis_index("gx")
     me_y = lax.axis_index("gy")
@@ -57,15 +63,12 @@
         pl.semaphore_signal(barrier, inc=1, device_id=device(offset), device_id_type=MESH)
 
     points = points_ref[...]
-    upper = points.astype(BF16).astype(F32)
-    lower = points - upper
-    main[13] = jnp.concatenate([upper[0:4], lower[0:3], upper[4:5]], axis=0).astype(BF16)
-    rest[13] = upper[5:6]
+    main[13] = jnp.concatenate([points, jnp.zeros((2, 512), F32)], axis=0).astype(BF16)
     pl.semaphore_wait(barrier, len(peers))
     copies = []
     for n, offset in enumerate(peers):
         slot = 26 - OFFSETS.index(offset)
-        for k, buffer in enumerate((main, rest)):
+        for k, buffer in enumerate((main,)):
             copy = pltpu.make_async_remote_copy(
                 src_ref=buffer.at[13],
                 dst_ref=buffer.at[slot],
@@ -112,16 +115,18 @@
     for t in range(8):
         moved = jnp.where(order + 128.0 * t == wide_rank, 1.0, 0.0).astype(BF16)
         moved = lax.dot_general(rows, moved, (((1,), (1,)), ((), ())), preferred_element_type=F32)
-        code = moved[32:64].astype(jnp.int32)
-        slots_ref[t] = moved[0:32].astype(jnp.int32) + 256 * (code & 1)
-        blocks_ref[t] = code >> 1
+        slots_ref[t] = moved[0:32].astype(jnp.int32)
+        blocks_ref[t] = moved[32:64].astype(jnp.int32)
         info_ref[t] = moved[64:72]
 
     for copy in copies:
         copy.wait_recv()
-    table_ref[0:216, :] = main[...].astype(F32).reshape(216, 512).astype(BF16)
-    tail = jnp.concatenate([rest[b] for b in range(27)] + [jnp.zeros((13, 512), F32)], axis=0)
-    table_ref[216:256, :] = tail.astype(BF16)
+    blocks = [main[b].astype(F32) for b in range(27)]
+    rows = [block[0:4] for block in blocks] + [block[4:6] for block in blocks]
+    rows.append(jnp.zeros((ROWS - SIX, 512), F32))
+    rows = jnp.concatenate(rows, axis=0).astype(BF16)
+    table_ref[0:ROWS, :] = rows[:, 0:256]
+    table_ref[ROWS : 2 * ROWS, :] = rows[:, 256:512]
     for copy in copies:
         copy.wait_send()
 
@@ -131,7 +136,7 @@
     return pl.pallas_call(
         halo_kernel,
         out_shape=[
-            jax.ShapeDtypeStruct((ROWS, 512), BF16),
+            jax.ShapeDtypeStruct((2 * ROWS, 256), BF16),
             jax.ShapeDtypeStruct((8, NB, 128), jnp.int32),
             jax.ShapeDtypeStruct((8, NB, 128), jnp.int32),
             jax.ShapeDtypeStruct((8, 8, 128), F32),
@@ -141,9 +146,8 @@
         out_specs=[vmem] * 5,
         scratch_shapes=[
             pltpu.VMEM((27, 8, 512), BF16),
-            pltpu.VMEM((27, 1, 512), F32),
-            pltpu.SemaphoreType.DMA((2, 26)),
-            pltpu.SemaphoreType.DMA((2, 26)),
+            pltpu.SemaphoreType.DMA((1, 26)),
+            pltpu.SemaphoreType.DMA((1, 26)),
         ],
         compiler_params=pltpu.CompilerParams(collective_id=1, has_side_effects=True),
     )(points, near, counts)
@@ -151,73 +155,97 @@
 
 def encoder_kernel(
     table_ref, slots_ref, blocks_ref, info_ref, rank_ref, in_ref, mid_ref, last_ref, out_ref,
-    first_scr, mid_scr, last_scr, ordered,
+    first_scr, mid_scr, last_scr, kept_scr, hidden_scr, base_scr, totals, trips,
 ):
     column = lax.broadcasted_iota(jnp.int32, (6, ROWS), 1)
     feature = lax.broadcasted_iota(jnp.int32, (6, ROWS), 0)
-    value = column % 8
-    wanted = jnp.where(value < 4, value, jnp.where(value == 7, 4, value - 4))
-    wanted = jnp.where(column >= 243, column - 243, jnp.where(column >= 216, 5, wanted))
-    chosen = jnp.where((feature == wanted) & (column < 246), 1.0, 0.0).astype(BF16)
+    wanted = jnp.where(column < FOUR, column % 4, 4 + column % 2)
+    wanted = jnp.where(column >= SIX, column - SIX, wanted)
+    chosen = jnp.where((feature == wanted) & (column < SIX + 3), 1.0, 0.0).astype(BF16)
     turn = (((0,), (0,)), ((), ()))
     first_scr[...] = lax.dot_general(in_ref[...], chosen, turn, preferred_element_type=F32).astype(BF16)
-    mid_scr[...] = (mid_ref[...].astype(F32).T * 0.5).astype(BF16)
+    half_mid = (mid_ref[...].astype(F32).T * 0.5).astype(BF16)
+    mid_scr[...] = jnp.zeros(mid_scr.shape, BF16)
+    mid_scr[0:80, 0:80] = half_mid
+    mid_scr[80:160, 80:160] = half_mid
     last_scr[...] = last_ref[...].astype(F32).T.astype(BF16)
 
-    slot_ids = lax.broadcasted_iota(jnp.int32, (512, 128), 0).astype(jnp.int16)
+    slot_ids = lax.broadcasted_iota(jnp.int32, (256, 128), 0).astype(jnp.int16)
     row = lax.broadcasted_iota(jnp.int32, (ROWS, 128), 0)
-    row_block = jnp.where(row < 216, row // 8, jnp.where(row < 243, row - 216, -1)).astype(jnp.int16)
-    zero = jnp.zeros((240, 128), BF16)
+    row_block = jnp.where(row < FOUR, row // 4, jnp.where(row < SIX, (row - FOUR) // 2, -1)).astype(jnp.int16)
     last_rows = lax.broadcasted_iota(jnp.int32, (16, 128), 0)
-
-    def chunk(c, carry):
-        lanes = pl.ds(pl.multiple_of(c * 128, 128), 128)
+    steps = 0
+    for c in range(8):
         info = info_ref[c]
-        counts = info[0:1]
-        most = jnp.max(counts).astype(jnp.int32)
+        trip = (jnp.max(info[0:1]).astype(jnp.int32) + SLOTS - 1) // SLOTS
+        trips[c] = trip
+        steps += trip
         centre = jnp.zeros((16, 128), F32)
         for d in range(3):
-            centre = jnp.where(last_rows == 3 + d, info[1 + d : 2 + d], centre)
-        base = jnp.concatenate([zero, centre.astype(BF16)], axis=0)
-
-        def step(t, total):
-            hot = []
-            for u in range(SLOTS):
-                slot = jnp.broadcast_to(slots_ref[c, pl.ds(SLOTS * t + u, 1), :], (16, 128)).astype(jnp.int16)
-                slot = jnp.concatenate([slot] * 32, axis=0)
-                hot.append(jnp.where(slot_ids == slot, BF16(1), BF16(0)))
-            found = jnp.dot(table_ref[...], jnp.concatenate(hot, axis=1), preferred_element_type=F32)
-            found = found.astype(BF16)
-            kept = []
-            for u in range(SLOTS):
-                block = jnp.broadcast_to(blocks_ref[c, pl.ds(SLOTS * t + u, 1), :], (16, 128)).astype(jnp.int16)
-                block = jnp.concatenate([block] * (ROWS // 16), axis=0)
-                kept.append(jnp.where(row_block == block, found[:, 128 * u : 128 * u + 128], base))
-            hidden = jnp.dot(first_scr[...], jnp.concatenate(kept, axis=1), preferred_element_type=F32)
-            hidden = twice_gelu(hidden).astype(BF16)
-            hidden = twice_gelu(jnp.dot(mid_scr[...], hidden, preferred_element_type=F32))
-            for u in range(SLOTS):
-                used = (SLOTS * t + u).astype(F32) < counts
-                total = total + jnp.where(used, hidden[:, 128 * u : 128 * u + 128], 0.0)
-            return total
-
-        total = lax.fori_loop(0, (most + SLOTS - 1) // SLOTS, step, jnp.zeros((80, 128), F32))
-        mean = total * (0.5 / counts)
+            centre = jnp.where(last_rows == SIX - ROWS + 16 + d, info[1 + d : 2 + d], centre)
+        base_scr[c] = centre.astype(BF16)
+        totals[c] = jnp.zeros((80, 128), F32)
+    totals[8] = jnp.zeros((80, 128), F32)
+    kept_scr[...] = jnp.zeros(kept_scr.shape, BF16)
+    hidden_scr[...] = jnp.zeros(hidden_scr.shape, BF16)
+
+    def step(n, places):
+        (c0, t0), (c1, t1), (c2, t2) = places
+        hidden = twice_gelu(jnp.dot(mid_scr[...], hidden_scr[...], preferred_element_type=F32))
+        counts = info_ref[jnp.minimum(c2, 7), 0:1, :]
+        total = totals[c2]
+        for u in range(SLOTS):
+            used = (SLOTS * t2 + u).astype(F32) < counts
+            here = hidden[80 * (u // 2) : 80 * (u // 2) + 80, 128 * (u % 2) : 128 * (u % 2) + 128]
+            total = total + jnp.where(used, here.astype(F32), 0.0)
+        totals[c2] = total
+        hidden = jnp.dot(first_scr[...], kept_scr[...], preferred_element_type=F32)
+        hidden = twice_gelu(hidden).astype(BF16)
+        for u in range(SLOTS // 2):
+            hidden_scr[80 * u : 80 * u + 80, :] = hidden[:, 256 * u : 256 * u + 256]
+        hot = []
+        for u in range(SLOTS):
+            slot = jnp.broadcast_to(slots_ref[c0, pl.ds(SLOTS * t0 + u, 1), :], (16, 128)).astype(jnp.int16)
+            slot = jnp.concatenate([slot] * 16, axis=0)
+            hot.append(jnp.where(slot_ids == slot, BF16(1), BF16(0)))
+        found = jnp.dot(table_ref[...], jnp.concatenate(hot, axis=1), preferred_element_type=F32)
+        found = found.astype(BF16)
+        for u in range(SLOTS):
+            code = jnp.broadcast_to(blocks_ref[c0, pl.ds(SLOTS * t0 + u, 1), :], (16, 128))
+            block = (code >> 1).astype(jnp.int16)
+            odd = (code & 1).astype(jnp.int16)
+            same = row_block == jnp.concatenate([block] * (ROWS // 16), axis=0)
+            odd = jnp.concatenate([odd] * (ROWS // 16), axis=0) == 1
+            here = found[:, 128 * u : 128 * u + 128]
+            here = jnp.where(odd, here[ROWS : 2 * ROWS], here[0:ROWS])
+            kept_scr[0 : ROWS - 16, 128 * u : 128 * u + 128] = jnp.where(same[0 : ROWS - 16], here[0 : ROWS - 16], BF16(0))
+            kept_scr[ROWS - 16 : ROWS, 128 * u : 128 * u + 128] = jnp.where(same[ROWS - 16 : ROWS], here[ROWS - 16 : ROWS], base_scr[c0])
+        ended = t0 + 1 >= trips[c0]
+        following = (
+            jnp.minimum(jnp.where(ended, c0 + 1, c0), 7),
+            jnp.where(ended, jnp.where(c0 == 7, t0, 0), t0 + 1),
+        )
+        return following, (c0, t0), (c1, t1)
+
+    start = (jnp.int32(0), jnp.int32(0))
+    spare = (jnp.int32(8), jnp.int32(0))
+    lax.fori_loop(0, steps + 2, step, (start, spare, spare))
+    last = last_scr[...]
+    ordered = []
+    for c in range(8):
+        mean = totals[c] * (0.5 / info_ref[c, 0:1, :])
         upper = mean.astype(BF16)
         lower = (mean - upper.astype(F32)).astype(BF16)
-        last = last_scr[...]
         values = jnp.dot(last, upper, preferred_element_type=F32) + jnp.dot(
             last, lower, preferred_element_type=F32
         )
-        ordered[:, lanes] = values.astype(BF16)
-        return carry
-
-    lax.fori_loop(0, 8, chunk, 0)
+        ordered.append(values.astype(BF16))
+    ordered = jnp.concatenate(ordered, axis=1)
     order = lax.broadcasted_iota(jnp.int32, (1024, 128), 0).astype(F32)
     parts = []
     for t in range(8):
         moved = jnp.where(order == rank_ref[0:1, 128 * t : 128 * t + 128], 1.0, 0.0).astype(BF16)
-        part = jnp.dot(ordered[...], moved, preferred_element_type=F32)
+        part = jnp.dot(ordered, moved, preferred_element_type=F32)
         parts.append(part.reshape(8, 8, 128))
     out_ref[...] = jnp.stack(parts, axis=1).reshape(8, 64, 128).astype(BF16)
 
@@ -231,9 +259,13 @@
         out_specs=vmem,
         scratch_shapes=[
             pltpu.VMEM((80, ROWS), BF16),
-            pltpu.VMEM((80, 80), BF16),
+            pltpu.VMEM((160, 160), BF16),
             pltpu.VMEM((64, 80), BF16),
-            pltpu.VMEM((64, 1024), BF16),
+            pltpu.VMEM((ROWS, 128 * SLOTS), BF16),
+            pltpu.VMEM((160, 256), BF16),
+            pltpu.VMEM((8, 16, 128), BF16),
+            pltpu.VMEM((9, 80, 128), F32),
+            pltpu.SMEM((8,), jnp.int32),
         ],
     )(table, slots, blocks, info, rank, kernel_in, kernel_mid, kernel_out)
 

time: 98 us -> 80 us (0.82)
  Pallas kernels: 93.2 us -> 75 us
    pallas_call x1, Pallas kernels: 31.8 us -> 15 us  [encode(): pl.pallas_call(encoder_kernel, out_shape=jax.ShapeDtypeStruct((8, 64, 128...]
where the time goes in v3:
time: 80 us; the launch traced here: 79.6 us
  Pallas kernels  75 us (94%)
  local copies, waits for them, and re-layouts  4.6 us (6%)
    pallas_call x1, Pallas kernels, spectral_layer(): pl.pallas_call(spectral_kernel, out_shape=jax.ShapeDtypeStruct((128, 8, 6...  42.9 us
    pallas_call x1, Pallas kernels, halo(): pl.pallas_call(halo_kernel, out_shape=[jax.ShapeDtypeStruct((2 * ROWS, 25...  17 us
    pallas_call x1, Pallas kernels, encode(): pl.pallas_call(encoder_kernel, out_shape=jax.ShapeDtypeStruct((8, 64, 128...  15 us
    unnamed x7, local copies, waits for them, and re-layouts  3.91 us

profile of v3, /device:TPU:1, one launch (start us, length us, event | category | flops | bytes accessed | tf_op | source)
XLA Modules:
  0.0 79.6 jit_solution(10834132036851028188)
XLA Ops:
  0.0 0.0 copy-start.1
  0.0 0.0 copy-start
  0.0 1.3 %copy.19 = f32[1,6,512]{2,1,0:T(8,128)} copy(f32[1,6,512]{2,0,1:T(1,128)} %param.14) | data formatting | bytes 24576
  1.3 0.0 copy-done.1
  1.3 0.7 copy.16.last_ref
  2.0 0.0 copy-done
  2.1 0.7 reshape.13.counts_ref
  2.7 17.0 %shard_map.136 = (bf16[352,256]{1,0:T(8,128)(2,1)}, s32[8,32,128]{2,1,0:T(8,128)}, s32[8,32,128]{2,1,0:T(8,128)}, f32[8,8,128]{2,1,0:T(8,128)}, f32[8,1024]{1,0:T(8,128)}) custom-call(f32[6,512]{1,0:T(8,128)} %bitcast.12, s32[1024,32]{1,0:T(8,128)} %bitcast.11, s32[1,1024]{1,0:T(1,128)} %reshape.13.counts_ref), custom_call_target="tpu_custom_call" | custom-call | tf_op jit(solution)/shard_map/pallas_call | solution.py:136
  19.8 15.0 %shard_map.137.latent_ref = bf16[8,64,128]{2,1,0:T(8,128)(2,1)} custom-call(bf16[352,256]{1,0:T(8,128)(2,1)} %get-tuple-element.10.table_ref, s32[8,32,128]{2,1,0:T(8,128)} %get-tuple-element.11.slots_ref, s32[8,32,128]{2,1,0:T(8,128)} %get-tuple-element.12.blocks_ref, f32[8,8,128]{2,1,0:T(8,128)} %get-tuple-element.13.info_ref, ...), custom_call_target="tpu_custom_call" | custom-call | tf_op jit(solution)/shard_map/pallas_call | solution.py:255
  34.8 42.9 %shard_map.138 = f32[128,8,64]{2,1,0:T(8,128)} custom-call(bf16[8,64,128]{2,1,0:T(8,128)(2,1)} %shard_map.137.latent_ref, bf16[64,64]{1,0:T(8,128)(2,1)} %skip_ref.1, bf16[2,16,64,64]{3,2,1,0:T(8,128)(2,1)} %bitcast.10, bf16[2,256,512]{2,1,0:T(8,128)(2,1)} %constant.12.clone.third_ref, bf16[2,512,256]{2,1,0:T(8,128)(2,1)} %constant.13.clone.back_ref, ...), custom_call_target="tpu_custom_call" | custom-call | tf_op jit(solution)/shard_map/pallas_call | solution.py:562
  77.7 1.9 %copy.21 = f32[1,8,16,8,64]{4,3,2,1,0:T(8,128)} copy(f32[1,8,16,8,64]{4,3,2,1,0:T(8,128)} %bitcast.9) | data formatting | bytes 524288
  (1 shorter events, 0.0 us)
Async XLA Ops:
  0.0 1.3 %copy-start.1 = (bf16[80,64]{0,1:T(8,128)(2,1)S(1)}, bf16[80,64]{0,1:T(8,128)(2,1)}, u32[]{:S(2)}) copy-start(bf16[80,64]{0,1:T(8,128)(2,1)} %param.19) | copy-start | bytes 30724
  0.0 2.0 %copy-start = (s32[1,8,16,8]{2,3,1,0:T(8,128)S(1)}, s32[1,8,16,8]{2,3,1,0:T(8,128)}, u32[]{:S(2)}) copy-start(s32[1,8,16,8]{2,3,1,0:T(8,128)} %param.16) | copy-start | bytes 12292

commit v4 on v3

--- a/solution.py
+++ b/solution.py
@@ -41,6 +41,13 @@
 OFFSETS = [(dx, dy, dz) for dx in (-1, 0, 1) for dy in (-1, 0, 1) for dz in (-1, 0, 1)]
 
 
+def regroup(back):
+    row = lax.broadcasted_iota(jnp.int32, (512, 512), 1 if back else 0)
+    column = lax.broadcasted_iota(jnp.int32, (512, 512), 0 if back else 1)
+    wanted = ((row >> 1) & 7) * 64 + (row >> 4) * 2 + (row & 1)
+    return jnp.where(wanted == column, 1.0, 0.0).astype(BF16)
+
+
 def halo_kernel(
     points_ref, near_ref, counts_ref, table_ref, slots_ref, blocks_ref, info_ref, rank_ref,
     main, send, recv,
@@ -62,8 +69,7 @@
     for offset in peers:
         pl.semaphore_signal(barrier, inc=1, device_id=device(offset), device_id_type=MESH)
 
-    points = points_ref[...]
-    main[13] = jnp.concatenate([points, jnp.zeros((2, 512), F32)], axis=0).astype(BF16)
+    main[13] = jnp.concatenate([points_ref[d] for d in range(6)] + [jnp.zeros((2, 512), F32)], axis=0).astype(BF16)
     pl.semaphore_wait(barrier, len(peers))
     copies = []
     for n, offset in enumerate(peers):
@@ -81,7 +87,8 @@
             copies.append(copy)
 
     lane = lax.broadcasted_iota(jnp.int32, (1, 1024), 1)
-    counts = counts_ref[...].astype(F32)
+    counts = jnp.concatenate([counts_ref[x].astype(F32) for x in range(8)], axis=1)
+    counts = jnp.concatenate([counts[z : z + 1] for z in range(8)], axis=1)
     key = counts * 1024.0 + (1023 - lane).astype(F32)
     ones = jnp.ones((8, 128), BF16)
     rank = jnp.zeros((8, 1024), F32)
@@ -168,7 +175,7 @@
     mid_scr[...] = jnp.zeros(mid_scr.shape, BF16)
     mid_scr[0:80, 0:80] = half_mid
     mid_scr[80:160, 80:160] = half_mid
-    last_scr[...] = last_ref[...].astype(F32).T.astype(BF16)
+    last_scr[...] = last_ref[...]
 
     slot_ids = lax.broadcasted_iota(jnp.int32, (256, 128), 0).astype(jnp.int16)
     row = lax.broadcasted_iota(jnp.int32, (ROWS, 128), 0)
@@ -245,16 +252,16 @@
     parts = []
     for t in range(8):
         moved = jnp.where(order == rank_ref[0:1, 128 * t : 128 * t + 128], 1.0, 0.0).astype(BF16)
-        part = jnp.dot(ordered, moved, preferred_element_type=F32)
-        parts.append(part.reshape(8, 8, 128))
-    out_ref[...] = jnp.stack(parts, axis=1).reshape(8, 64, 128).astype(BF16)
+        parts.append(jnp.dot(ordered, moved, preferred_element_type=F32).astype(BF16))
+    parts = jnp.dot(regroup(False), jnp.concatenate(parts, axis=0), preferred_element_type=F32)
+    out_ref[...] = parts.astype(BF16).reshape(32, 16, 128)
 
 
 def encode(table, slots, blocks, info, rank, kernel_in, kernel_mid, kernel_out):
     vmem = pl.BlockSpec(memory_space=pltpu.VMEM)
     return pl.pallas_call(
         encoder_kernel,
-        out_shape=jax.ShapeDtypeStruct((8, 64, 128), BF16),
+        out_shape=jax.ShapeDtypeStruct((32, 16, 128), BF16),
         in_specs=[vmem] * 8,
         out_specs=vmem,
         scratch_shapes=[
@@ -292,9 +299,8 @@
 @functools.lru_cache(None)
 def third_table():
     cos, sin = turn(np.arange(16)[:, None], np.arange(64)[None, :])
-    parts = np.stack([cos, -sin]).reshape(2, 4, 4, 64).transpose(1, 0, 2, 3)
-    full = np.einsum("arkz,cd->arkczd", parts, np.eye(8))
-    return full.reshape(256, 512)
+    full = np.einsum("akz,cd->akczd", np.stack([cos, -sin]), np.eye(2))
+    return full.reshape(64, 128)
 
 
 @functools.lru_cache(None)
@@ -351,42 +357,38 @@
 def spectral_kernel(
     latent_ref, skip_ref, weight_ref, third_ref, back_ref, second_ref, first_ref, firstt_ref, pair_ref,
     out_ref,
-    r1, z_msg, r2, s_msg, r3, t_msg, r4, mixing, n_msg, r5, g_msg, r6, f_msg, v_msg, r7, rv, b_msg, r8, skip,
-    send, recv,
+    r1, w_msg, rw, s_msg, r3, mixing, n_msg, r5, g_msg, r6, b_msg, r8, skip, send, recv,
 ):
     me_x = lax.axis_index("gx")
     me_y = lax.axis_index("gy")
     me_z = lax.axis_index("gz")
-    mine = {"gx": me_x, "gy": me_y, "gz": me_z}
-    sizes = {"gx": GX, "gy": GY, "gz": GZ}
-
+    me_q = me_y * GZ + me_z
+    columns = [(y, z) for y in range(GY) for z in range(GZ) if y or z]
+
+    def across(o):
+        y, z = lax.rem(me_y + o[0], GY), lax.rem(me_z + o[1], GZ)
+        return o[0] * GZ + o[1], {"gy": y, "gz": z}, y * GZ + z, me_q
+
+    def along_x(o):
+        peer = lax.rem(me_x + o, GX)
+        return o, {"gx": peer}, peer, me_x
+
+    planes = [across(o) for o in columns]
+    lines = [along_x(o) for o in range(1, GX)]
     barrier = pltpu.get_barrier_semaphore()
-    total = 0
-    for axis in ("gz", "gy", "gx"):
-        for o in range(1, sizes[axis]):
-            pl.semaphore_signal(
-                barrier, inc=1, device_id={axis: lax.rem(mine[axis] + o, sizes[axis])}, device_id_type=MESH
-            )
-            total += 1
-    pl.semaphore_wait(barrier, total)
-
-    same = lax.broadcasted_iota(jnp.int32, (128, 128), 0) // 16 == lax.broadcasted_iota(jnp.int32, (128, 128), 1) // 16
-
-    def spread_blocks(ref, part, l):
-        small = ref[me_x, part, l].astype(F32)
-        return jnp.where(same, jnp.concatenate([small] * 8, axis=0), 0.0).astype(BF16)
-
-    def start(stage, axis, source, target):
+    for _, device, _, _ in planes + lines:
+        pl.semaphore_signal(barrier, inc=1, device_id=device, device_id_type=MESH)
+    pl.semaphore_wait(barrier, len(planes + lines))
+
+    def start(stage, peers, source, target):
         copies = []
-        size = sizes[axis]
-        for o in range(1, size):
-            peer = lax.rem(mine[axis] + o, size)
+        for n, device, peer, me in peers:
             copy = pltpu.make_async_remote_copy(
                 src_ref=source(peer),
-                dst_ref=target.at[mine[axis]],
-                send_sem=send.at[stage, o],
-                recv_sem=recv.at[stage, o],
-                device_id={axis: peer},
+                dst_ref=target.at[me],
+                send_sem=send.at[stage, n],
+                recv_sem=recv.at[stage, n],
+                device_id=device,
                 device_id_type=MESH,
             )
             copy.start()
@@ -398,33 +400,40 @@
             copy.wait_recv()
 
     waiting = []
-
-    first = start(0, "gz", lambda p: latent_ref.at[p], r1)
+    rows128 = lax.broadcasted_iota(jnp.int32, (128, 128), 0)
+    lanes128 = lax.broadcasted_iota(jnp.int32, (128, 128), 1)
+    same = rows128 // 16 == lanes128 // 16
+
+    def spread_blocks(ref, part, l):
+        small = ref[me_x, part, l].astype(F32)
+        return jnp.where(same, jnp.concatenate([small] * 8, axis=0), 0.0).astype(BF16)
+
+    first = start(0, planes, lambda p: latent_ref.at[p], r1)
     waiting += first
-    r1[me_z] = latent_ref[me_z]
+    r1[me_q] = latent_ref[me_q]
+    forth = regroup(False)
+    for l in range(2):
+        wide = jnp.concatenate(
+            [weight_ref[b, 8 * l : 8 * l + 8].astype(F32).reshape(512, 64) for b in range(2)], axis=1
+        ).astype(BF16)
+        w_msg[:, 16 * l : 16 * l + 16, :] = dotf(forth, wide).astype(BF16).reshape(32, 16, 128)
+    weights = start(1, planes, lambda p: w_msg.at[p], rw)
+    waiting += weights
+    rw[me_q] = w_msg[me_q]
     first_tab = [[spread_blocks(first_ref, p, l) for l in range(2)] for p in range(2)]
     back_tab = [[spread_blocks(firstt_ref, p, l) for l in range(2)] for p in range(2)]
     skip_t = skip_ref[...].astype(F32).T.astype(BF16)
+    natural = dotf(regroup(True), latent_ref[...].reshape(512, 128)).astype(BF16)
     for z in range(8):
-        here = latent_ref[:, 8 * z : 8 * z + 8, :].reshape(64, 128)
-        skip[z] = dotf(skip_t, here)
-    for s in range(8):
-        halves_of = []
-        for b in range(2):
-            halves_of.append(weight_ref[b, :, 8 * s : 8 * s + 8, :].astype(F32).reshape(128, 64))
-        mixing[128 * s : 128 * s + 128, :] = jnp.concatenate(halves_of, axis=1).astype(BF16)
+        skip[z] = dotf(skip_t, natural[64 * z : 64 * z + 64])
     finish(first)
-    values = r1[...].reshape(512, 128)
-    spectrum = dotf(third_ref[0], values) + dotf(third_ref[1], values)
-    z_msg[...] = spectrum.astype(BF16).reshape(4, 64, 128)
-
-    second = start(1, "gy", lambda p: z_msg.at[p], r2)
-    waiting += second
-    r2[me_y] = z_msg[me_y]
-    finish(second)
-    wide = jnp.concatenate(
-        [r2[e, 32 * b : 32 * b + 32, :] for e in range(4) for b in range(2)], axis=1
-    )
+
+    pieces = []
+    for e in range(4):
+        values = r1[8 * e : 8 * e + 8].reshape(128, 128)
+        piece = dotf(third_ref[0], values) + dotf(third_ref[1], values)
+        pieces += [piece[0:32], piece[32:64]]
+    wide = jnp.concatenate(pieces, axis=1).astype(BF16)
     rows = jnp.concatenate(
         [dott(second_ref[0, l], wide) + dott(second_ref[1, l], wide) for l in range(2)], axis=1
     )
@@ -438,61 +447,57 @@
     )
     s_msg[...] = partial.astype(BF16).reshape(8, 16, 128)
 
-    third = start(2, "gx", lambda p: s_msg.at[p], r3)
+    third = start(2, lines, lambda p: s_msg.at[p], r3)
     waiting += third
     r3[me_x] = s_msg[me_x]
+    finish(weights)
+    for h in range(8):
+        parts = [
+            rw[e * 8 + h, 8 * p : 8 * p + 8, :].astype(F32) for p in range(4) for e in range(4)
+        ]
+        mixing[h] = jnp.concatenate(parts, axis=0).astype(BF16)
     finish(third)
     modes = jnp.sum(r3[...].astype(F32), axis=0)
+
+    rows64 = lax.broadcasted_iota(jnp.int32, (64, 128), 0)
+    lanes64 = lax.broadcasted_iota(jnp.int32, (64, 128), 1)
+    own = rows64 == lanes64 // 2
+    spread = jnp.where(own, 1.0, 0.0).astype(BF16)
+    sign = jnp.where(lanes64 < 64, -1.0, 1.0)
+    pair_same = rows128 % 2 == lanes128 % 2
+    fold = jnp.where((rows64 % 2) * 32 + rows64 // 2 == lanes64 // 2, 1.0, 0.0).astype(BF16)
+    turned = []
     for h in range(8):
-        t_msg[h] = modes[2 * h : 2 * h + 2, :]
-
-    fourth = start(3, "gz", lambda p: t_msg.at[p], r4)
+        expanded = jnp.concatenate(
+            [
+                jnp.where(own, jnp.broadcast_to(modes[2 * h + a : 2 * h + a + 1], (64, 128)), 0.0)
+                for a in range(2)
+            ],
+            axis=0,
+        ).astype(BF16)
+        product = dotf(expanded, mixing[h])
+        mixed = product[0:64] + pltpu.roll(product[64:128], 64, 1) * sign
+        tall = lax.dot_general(
+            mixed.astype(BF16), spread, (((0,), (0,)), ((), ())), preferred_element_type=F32
+        )
+        tall = jnp.where(pair_same, tall, 0.0).astype(BF16)
+        turned.append(dotf(fold, tall).astype(BF16))
+    n_msg[...] = dotf(forth, jnp.concatenate(turned, axis=0)).astype(BF16).reshape(32, 16, 128)
+
+    fourth = start(3, planes, lambda p: n_msg.at[p], r5)
     waiting += fourth
-    r4[me_z] = t_msg[me_z]
+    r5[me_q] = n_msg[me_q]
     finish(fourth)
-    mode_rows = lax.broadcasted_iota(jnp.int32, (16, 128), 0)
-    lanes16 = lax.broadcasted_iota(jnp.int32, (16, 128), 1)
-    own = mode_rows == lanes16 // 8
-    expanded = jnp.concatenate(
-        [
-            jnp.concatenate(
-                [
-                    jnp.where(own, jnp.broadcast_to(r4[s, a : a + 1, :], (16, 128)), 0.0)
-                    for s in range(8)
-                ],
-                axis=1,
-            )
-            for a in range(2)
-        ],
-        axis=0,
-    ).astype(BF16)
-    product = dotf(expanded, mixing[...])
-    sign = jnp.where(lanes16 < 64, -1.0, 1.0)
-    mixed = product[0:16] + pltpu.roll(product[16:32], 64, 1) * sign
-    first_place = (me_x + me_y + me_z) == 0
-    mixed = jnp.where((mode_rows == 0) & first_place, 0.0, mixed)
-    spread = jnp.where(own, 1.0, 0.0).astype(BF16)
-    tall = lax.dot_general(
-        mixed.astype(BF16), spread, (((0,), (0,)), ((), ())), preferred_element_type=F32
-    )
-    tall_rows = lax.broadcasted_iota(jnp.int32, (128, 128), 0)
-    tall_lanes = lax.broadcasted_iota(jnp.int32, (128, 128), 1)
-    tall = jnp.where(tall_rows % 8 == tall_lanes % 8, tall, 0.0).astype(BF16)
-    gather = (mode_rows % 2) * 8 + mode_rows // 2 == lanes16 // 8
-    turned = dotf(jnp.where(gather, 1.0, 0.0).astype(BF16), tall)
-    for h in range(8):
-        n_msg[h] = turned[2 * h : 2 * h + 2, :]
-
-    fifth = start(4, "gz", lambda p: n_msg.at[p], r5)
+    mixed = jnp.sum(r5[...].astype(F32), axis=0)
+    zero_rows = lax.broadcasted_iota(jnp.int32, (16, 128), 0)
+    zero_lanes = lax.broadcasted_iota(jnp.int32, (16, 128), 1)
+    mixed = jnp.where((zero_rows < 2) & (zero_lanes < 2) & (me_x == 0), 0.0, mixed)
+    g_msg[...] = mixed.astype(BF16)
+
+    fifth = start(4, lines, lambda p: g_msg, r6)
     waiting += fifth
-    r5[me_z] = n_msg[me_z]
+    r6[me_x] = g_msg[...]
     finish(fifth)
-    g_msg[...] = jnp.concatenate([r5[h] for h in range(8)], axis=0).astype(BF16)
-
-    sixth = start(5, "gx", lambda p: g_msg, r6)
-    waiting += sixth
-    r6[me_x] = g_msg[...]
-    finish(sixth)
     field = r6[...].reshape(128, 128)
     along = (
         dotf(back_tab[0][0], field[:, 0:64])
@@ -509,55 +514,39 @@
         + dotf(lower[32:64], second_ref[0, 1])
         + dotf(upper[32:64], second_ref[1, 1])
     )
-    zero_rows = lax.broadcasted_iota(jnp.int32, (32, 1024), 0)
     scale = 1.0 / GRID**3
-    plane = plane * jnp.where((zero_rows < 8) & (me_y == 0), scale, 2.0 * scale)
-    for e in range(4):
-        for b in range(2):
-            part = plane[:, (2 * e + b) * 128 : (2 * e + b + 1) * 128]
-            f_msg[e, 32 * b : 32 * b + 32, :] = part.astype(BF16)
-
-    seventh = start(6, "gy", lambda p: f_msg.at[p], r7)
-    waiting += seventh
-    r7[me_y] = f_msg[me_y]
+    plane_rows = lax.broadcasted_iota(jnp.int32, (32, 1024), 0)
+    plane = (plane * jnp.where(plane_rows < 2, scale, 2.0 * scale)).astype(BF16)
     wide_field = field.astype(F32)
-    lane_group = tall_lanes // 32
     paired = jnp.zeros((128, 128), F32)
     for p in range(4):
-        paired = jnp.where(lane_group == p, dotf(pair_ref[p], field), paired)
-    low = ((tall_lanes // 8) % 4 == 0) & (me_y == 0)
+        paired = jnp.where(lanes128 // 32 == p, dotf(pair_ref[p], field), paired)
+    low = (lanes128 // 2) % 16 == 0
     power = jnp.where(low, 0.5 * wide_field * (wide_field + paired), 2.0 * wide_field * wide_field)
     power = jnp.sum(power, axis=0, keepdims=True)
-    power = power + pltpu.roll(power, 64, 1)
-    power = power + pltpu.roll(power, 32, 1)
-    power = power + pltpu.roll(power, 16, 1)
-    power = power + pltpu.roll(power, 8, 1)
-    tall_power = jnp.broadcast_to(power, (128, 128)).T
-    v_msg[...] = tall_power[0:8, :] * (scale * scale)
-    eighth = start(7, "gy", lambda p: v_msg, rv)
-    waiting += eighth
-    rv[me_y] = v_msg[...]
-    finish(seventh)
-    grid_part = r7[...].reshape(256, 128)
-    branch = dotf(back_ref[0], grid_part) + dotf(back_ref[1], grid_part)
-    finish(eighth)
-    variance = (rv[0] + rv[1]) + (rv[2] + rv[3])
+    for shift in (64, 32, 16, 8, 4, 2):
+        power = power + pltpu.roll(power, shift, 1)
+    variance = jnp.broadcast_to(power, (128, 128)).T * (scale * scale)
     inverse = 1.0 / jnp.sqrt(variance + NORM_FLOOR)
-    branch = branch.reshape(64, 8, 128) * inverse[None]
-    b_msg[...] = branch.reshape(8, 64, 128).astype(BF16)
-
-    ninth = start(8, "gz", lambda p: b_msg.at[p], r8)
-    waiting += ninth
-    r8[me_z] = b_msg[me_z]
-    finish(ninth)
+    for e in range(4):
+        part = jnp.concatenate(
+            [plane[:, (2 * e + b) * 128 : (2 * e + b + 1) * 128] for b in range(2)], axis=0
+        )
+        branch = (dotf(back_ref[0], part) + dotf(back_ref[1], part)) * inverse
+        b_msg[8 * e : 8 * e + 8] = branch.astype(BF16).reshape(8, 16, 128)
+
+    sixth = start(5, planes, lambda p: b_msg.at[p], r8)
+    waiting += sixth
+    r8[me_q] = b_msg[me_q]
+    finish(sixth)
+    normed = dotf(regroup(True), r8[...].reshape(512, 128))
     for z in range(8):
-        normed = r8[:, 8 * z : 8 * z + 8, :].astype(F32).reshape(64, 128)
-        out_ref[:, z, :] = gelu(normed + skip[z]).T
+        out_ref[:, z, :] = gelu(normed[64 * z : 64 * z + 64] + skip[z]).T
     for copy in waiting:
         copy.wait_send()
 
 
-def spectral_layer(latent, skip_t, weight, third, back, second, first, firstt, pair):
+def spectral_layer(latent, skip_w, weight, third, back, second, first, firstt, pair):
     vmem = pl.BlockSpec(memory_space=pltpu.VMEM)
     return pl.pallas_call(
         spectral_kernel,
@@ -565,40 +554,34 @@
         in_specs=[vmem] * 9,
         out_specs=vmem,
         scratch_shapes=[
-            pltpu.VMEM((8, 64, 128), BF16),
-            pltpu.VMEM((4, 64, 128), BF16),
-            pltpu.VMEM((4, 64, 128), BF16),
+            pltpu.VMEM((32, 16, 128), BF16),
+            pltpu.VMEM((32, 32, 128), BF16),
+            pltpu.VMEM((32, 32, 128), BF16),
             pltpu.VMEM((8, 16, 128), BF16),
             pltpu.VMEM((8, 16, 128), BF16),
-            pltpu.VMEM((8, 2, 128), F32),
-            pltpu.VMEM((8, 2, 128), F32),
-            pltpu.VMEM((1024, 128), BF16),
-            pltpu.VMEM((8, 2, 128), F32),
-            pltpu.VMEM((8, 2, 128), F32),
+            pltpu.VMEM((8, 128, 128), BF16),
+            pltpu.VMEM((32, 16, 128), BF16),
+            pltpu.VMEM((32, 16, 128), BF16),
             pltpu.VMEM((16, 128), BF16),
             pltpu.VMEM((8, 16, 128), BF16),
-            pltpu.VMEM((4, 64, 128), BF16),
-            pltpu.VMEM((8, 128), F32),
-            pltpu.VMEM((4, 64, 128), BF16),
-            pltpu.VMEM((4, 8, 128), F32),
-            pltpu.VMEM((8, 64, 128), BF16),
-            pltpu.VMEM((8, 64, 128), BF16),
+            pltpu.VMEM((32, 16, 128), BF16),
+            pltpu.VMEM((32, 16, 128), BF16),
             pltpu.VMEM((8, 64, 128), F32),
-            pltpu.SemaphoreType.DMA((9, 8)),
-            pltpu.SemaphoreType.DMA((9, 8)),
+            pltpu.SemaphoreType.DMA((6, 32)),
+            pltpu.SemaphoreType.DMA((6, 32)),
         ],
         compiler_params=pltpu.CompilerParams(collective_id=0, has_side_effects=True),
-    )(latent, skip_t, weight, third, back, second, first, firstt, pair)
+    )(latent, skip_w, weight, third, back, second, first, firstt, pair)
 
 
 def body(point_data, neighbours, counts, kernel_in, kernel_mid, kernel_out, spectral, skip_weight):
     cells_x, cells_y, cells_z = neighbours.shape[1:4]
     made = halo(
-        point_data[0],
+        jnp.transpose(point_data, (1, 0, 2)),
         neighbours.reshape(-1, NB),
-        jnp.transpose(counts[0], (2, 0, 1)).reshape(1, -1),
+        jnp.transpose(counts[0], (0, 2, 1)),
     )
-    latent = encode(*made, kernel_in, kernel_mid, kernel_out)
+    latent = encode(*made, kernel_in, kernel_mid, kernel_out.T)
     third = third_table()
     by_place = first_table()
     out = spectral_layer(

time: 80 us -> 75.5 us (0.944)
  local copies, waits for them, and re-layouts: 4.6 us -> 1.87 us
  Pallas kernels: 75 us -> 73.3 us
    pallas_call x1, Pallas kernels: 42.9 us -> 40.7 us  [spectral_layer(): pl.pallas_call(spectral_kernel, out_shape=jax.ShapeDtypeStruct((128, 8, 6...]
    unnamed x7 -> x1, local copies, waits for them, and re-layouts: 3.91 us -> 1.87 us
where the time goes in v4:
time: 75.5 us; the launch traced here: 75.2 us
  Pallas kernels  73.3 us (97%)
  local copies, waits for them, and re-layouts  1.87 us (2%)
    pallas_call x1, Pallas kernels, spectral_layer(): pl.pallas_call(spectral_kernel, out_shape=jax.ShapeDtypeStruct((128, 8, 6...  40.7 us
    pallas_call x1, Pallas kernels, halo(): pl.pallas_call(halo_kernel, out_shape=[jax.ShapeDtypeStruct((2 * ROWS, 25...  17 us
    pallas_call x1, Pallas kernels, encode(): pl.pallas_call(encoder_kernel, out_shape=jax.ShapeDtypeStruct((32, 16, 12...  15.6 us
    unnamed x1, local copies, waits for them, and re-layouts  1.87 us

profile of v4, /device:TPU:1, one launch (start us, length us, event | category | flops | bytes accessed | tf_op | source)
XLA Modules:
  0.0 75.2 jit_solution(17174028617363395566)
XLA Ops:
  0.0 17.0 %shard_map.136 = (bf16[352,256]{1,0:T(8,128)(2,1)}, s32[8,32,128]{2,1,0:T(8,128)}, s32[8,32,128]{2,1,0:T(8,128)}, f32[8,8,128]{2,1,0:T(8,128)}, f32[8,1024]{1,0:T(8,128)}) custom-call(f32[6,1,512]{2,1,0:T(1,128)} %bitcast.13, s32[1024,32]{1,0:T(8,128)} %bitcast.9, s32[8,8,16]{2,1,0:T(8,128)} %bitcast.11), custom_call_target="tpu_custom_call" | custom-call | tf_op jit(solution)/shard_map/pallas_call | solution.py:143
  17.0 15.6 %shard_map.137.latent_ref = bf16[32,16,128]{2,1,0:T(8,128)(2,1)} custom-call(bf16[352,256]{1,0:T(8,128)(2,1)} %get-tuple-element.10.table_ref, s32[8,32,128]{2,1,0:T(8,128)} %get-tuple-element.11.slots_ref, s32[8,32,128]{2,1,0:T(8,128)} %get-tuple-element.12.blocks_ref, f32[8,8,128]{2,1,0:T(8,128)} %get-tuple-element.13.info_ref, ...), custom_call_target="tpu_custom_call" | custom-call | tf_op jit(solution)/shard_map/pallas_call | solution.py:262
  32.7 40.7 %shard_map.138 = f32[128,8,64]{2,1,0:T(8,128)} custom-call(bf16[32,16,128]{2,1,0:T(8,128)(2,1)} %shard_map.137.latent_ref, bf16[64,64]{1,0:T(8,128)(2,1)} %skip_ref.1, bf16[2,16,64,64]{3,2,1,0:T(8,128)(2,1)} %bitcast.10, bf16[2,64,128]{2,1,0:T(8,128)(2,1)} %constant.12.clone.third_ref, bf16[2,128,64]{2,1,0:T(8,128)(2,1)} %constant.13.clone.back_ref, ...), custom_call_target="tpu_custom_call" | custom-call | tf_op jit(solution)/shard_map/pallas_call | solution.py:551
  73.3 1.9 %copy.16 = f32[1,8,16,8,64]{4,3,2,1,0:T(8,128)} copy(f32[1,8,16,8,64]{4,3,2,1,0:T(8,128)} %bitcast.8) | data formatting | bytes 524288
